TPU v7x, 32 devices: a whole 2x2x4 slice. The times are simulated.
32 devices in a mesh: dp: 8 (over y, x, core), tp: 4 (over z).
Axes of the slice: x: 2, y: 2, z: 4, core: 2. Of those that a mesh axis runs over, the one named last changes fastest.
Arguments:
- tokens: bfloat16 [32768, 768], P('dp'), may hold values from -6 to 6
- cotangent: bfloat16 [32768, 768], P('dp'), may hold values from -6 to 6
- size_tags: int32 [8], P('dp'), may hold values from 0 to 1
- time_index: int32 [32], replicated, may hold values from 0 to 999
- class_index: int32 [32], replicated, may hold values from 0 to 999
- time_table: bfloat16 [1000, 768], replicated, may hold values from -6 to 6
- class_table: bfloat16 [1000, 768], replicated, may hold values from -6 to 6
- w_mod: bfloat16 [768, 4608], P(None, 'tp'), may hold values from -0.21875 to 0.21875
- w_qkv: bfloat16 [768, 2304], P(None, 'tp'), may hold values from -0.21875 to 0.21875
- conv_qkv: bfloat16 [9, 2304], P(None, 'tp'), may hold values from -2 to 2
- w_out: bfloat16 [768, 768], P('tp'), may hold values from -0.75 to 0.75
- w_up: bfloat16 [768, 3072], P(None, 'tp'), may hold values from -0.21875 to 0.21875
- conv_ffn: bfloat16 [9, 3072], P(None, 'tp'), may hold values from -2 to 2
- w_down: bfloat16 [3072, 768], P('tp'), may hold values from -0.109375 to 0.109375
Outputs:
- mixed: bfloat16 [32768, 768], P('dp')
- grad_tokens: float32 [32768, 768], P(('dp', 'tp'))
- grad_time: float32 [1000, 768], P(None, 'dp')
- grad_class: float32 [1000, 768], P(None, 'dp')
- grad_mod: float32 [768, 4608], P('dp', 'tp')
- grad_qkv: float32 [768, 2304], P('dp', 'tp')
- grad_conv_qkv: float32 [9, 2304], P(None, ('tp', 'dp'))
- grad_out: float32 [768, 768], P('tp', 'dp')
- grad_up: float32 [768, 3072], P('dp', 'tp')
- grad_conv_ffn: float32 [9, 3072], P(None, ('tp', 'dp'))
- grad_down: float32 [3072, 768], P('tp', 'dp')
Inputs may be any that keep to these rules, and one draw needn't show every extreme that they name: `size_tags`: 1: the buffer holds one item of 64 x 64 tokens and only its slot 0 is used; 0: four items, one in each quadrant of the grid, in slots of quadrant order.
All inputs are finite; a program needn't handle non-finite values.
Results may differ from a plain program's by a relative error of at most 0.018.
The roundings to bfloat16 on the way count: a program that leaves them out, or rounds other values in their place, can miss the bound.
Values may be sent and summed in bfloat16 or wider, within the bound.
A program may use at most 384 MiB of HBM per device.

v0:
```python
from functools import partial

import jax
import jax.numpy as jnp
from jax import lax
from jax.sharding import PartitionSpec as P

D = 768
HEAD_SIZE = 64
SIDE = 64
SLOTS = 4


def layer_norm(values):
    average = jnp.mean(values, axis=-1, keepdims=True)
    centred = values - average
    variance = jnp.mean(centred * centred, axis=-1, keepdims=True)
    return centred * lax.rsqrt(variance + 1e-06)


def item_ids(size_tag, grid_side):
    row_index = lax.broadcasted_iota(jnp.int32, (grid_side, grid_side), 0)
    col_index = lax.broadcasted_iota(jnp.int32, (grid_side, grid_side), 1)
    quadrant = row_index // (grid_side // 2) * 2 + col_index // (grid_side // 2)
    return jnp.where(size_tag == 1, jnp.zeros_like(quadrant), quadrant)


def depthwise(field, kernel, labels):
    grid_side = field.shape[0]
    padded = jnp.pad(field, ((1, 1), (1, 1), (0, 0)))
    padded_ids = jnp.pad(labels, 1, constant_values=-1)
    result = jnp.zeros_like(field)
    for tap_index in range(9):
        row_off = tap_index // 3
        col_off = tap_index % 3
        moved = padded[row_off : row_off + grid_side, col_off : col_off + grid_side]
        same_item = (
            padded_ids[row_off : row_off + grid_side, col_off : col_off + grid_side] == labels
        )
        result = result + kernel[tap_index] * jnp.where(
            same_item[:, :, None], moved, jnp.zeros_like(moved)
        )
    return result


def unshuffle(field):
    half_side = field.shape[0] // 2
    trailing = field.shape[2:]
    shaped = field.reshape((half_side, 2, half_side, 2) + trailing)
    order = (1, 3, 0, 2) + tuple(range(4, 4 + len(trailing)))
    return shaped.transpose(order).reshape((4, half_side * half_side) + trailing)


def shuffle(groups, grid_side):
    half_side = grid_side // 2
    trailing = groups.shape[2:]
    shaped = groups.reshape((2, 2, half_side, half_side) + trailing)
    order = (2, 0, 3, 1) + tuple(range(4, 4 + len(trailing)))
    return shaped.transpose(order).reshape((grid_side, grid_side) + trailing)


def attend(input_query, input_keys, input_values, allowed):
    scale_factor = HEAD_SIZE ** (-0.5)
    logit_scores = (
        jnp.einsum("yoe,goe->oyg", input_query, input_keys, preferred_element_type=jnp.float32)
        * scale_factor
    )
    logit_scores = jnp.where(allowed[None], logit_scores, -jnp.inf)
    row_top = jnp.max(logit_scores, axis=-1, keepdims=True)
    expo = jnp.exp(logit_scores - row_top)
    totals = jnp.sum(expo, axis=-1, keepdims=True)
    probabilities = (expo / totals).astype(jnp.bfloat16)
    result = jnp.einsum(
        "xbg,gxy->bxy", probabilities, input_values, preferred_element_type=jnp.float32
    ).astype(jnp.bfloat16)
    log_sums = (row_top + jnp.log(totals))[:, :, 0].T
    return (result, log_sums)


def attend_back(input_query, input_keys, input_values, allowed, gradient_result, log_sums):
    scale_factor = HEAD_SIZE ** (-0.5)
    logit_scores = (
        jnp.einsum("yoe,goe->oyg", input_query, input_keys, preferred_element_type=jnp.float32)
        * scale_factor
    )
    logit_scores = jnp.where(allowed[None], logit_scores, -jnp.inf)
    probabilities = jnp.exp(logit_scores - log_sums.T[:, :, None])
    grad_probs = jnp.einsum(
        "yoe,goe->oyg", gradient_result, input_values, preferred_element_type=jnp.float32
    )
    row_dots = jnp.sum(grad_probs * probabilities, axis=-1, keepdims=True)
    gradient_scores = (probabilities * (grad_probs - row_dots)).astype(jnp.bfloat16)
    grad_query = (
        jnp.einsum("xbg,gxy->bxy", gradient_scores, input_keys, preferred_element_type=jnp.float32)
        * scale_factor
    )
    grad_keys = (
        jnp.einsum("zew,ezb->wzb", gradient_scores, input_query, preferred_element_type=jnp.float32)
        * scale_factor
    )
    grad_values = jnp.einsum(
        "zew,ezb->wzb",
        probabilities.astype(jnp.bfloat16),
        gradient_result,
        preferred_element_type=jnp.float32,
    )
    return jnp.stack([grad_query, grad_keys, grad_values], axis=2)


def group_forward(block, allowed, size_tag):
    input_query = block[:, :, 0]
    input_keys = block[:, :, 1]
    input_values = block[:, :, 2]
    return attend(input_query, input_keys, input_values, allowed)


def group_backward(operands, allowed, size_tag):
    block, grad_block, log_sums = operands
    input_query = block[:, :, 0]
    input_keys = block[:, :, 1]
    input_values = block[:, :, 2]
    return attend_back(input_query, input_keys, input_values, allowed, grad_block, log_sums)


def modulate(values, shift_part, scale_part):
    return layer_norm(values) * (1.0 + scale_part) + shift_part


def per_device(
    tokens,
    cotangent,
    size_tags,
    time_index,
    class_index,
    time_table,
    class_table,
    w_mod,
    w_qkv,
    conv_qkv,
    w_out,
    w_up,
    conv_ffn,
    w_down,
):
    tp_count = lax.axis_size("tp")
    tp_rank = lax.axis_index("tp")
    dp_rank = lax.axis_index("dp")
    size_tag = size_tags[0]
    tok_count = tokens.shape[0]
    half_side = SIDE // 2
    heads_dev = w_out.shape[0] // HEAD_SIZE
    qkv_width = w_qkv.shape[1]
    hidden_width = w_up.shape[1]
    my_times = lax.dynamic_slice_in_dim(time_index, dp_rank * SLOTS, SLOTS)
    my_labels = lax.dynamic_slice_in_dim(class_index, dp_rank * SLOTS, SLOTS)
    condition = jnp.take(time_table, my_times, axis=0).astype(jnp.float32) + jnp.take(
        class_table, my_labels, axis=0
    ).astype(jnp.float32)
    activated = jax.nn.silu(condition).astype(jnp.bfloat16)
    mod_part = jnp.dot(activated, w_mod, preferred_element_type=jnp.float32)
    modulation = lax.all_gather(mod_part, "tp", axis=1, tiled=True)
    per_quad = jnp.where(
        size_tag == 1, jnp.broadcast_to(modulation[0:1], modulation.shape), modulation
    )
    quad_grid = per_quad.reshape(2, 1, 2, 1, 6 * D)
    shift_one = quad_grid[..., 0:D]
    scale_one = quad_grid[..., D : 2 * D]
    gate_one = quad_grid[..., 2 * D : 3 * D]
    shift_two = quad_grid[..., 3 * D : 4 * D]
    scale_two = quad_grid[..., 4 * D : 5 * D]
    gate_two = quad_grid[..., 5 * D : 6 * D]
    labels_grid = item_ids(size_tag, SIDE)
    group_labels = item_ids(size_tag, half_side).reshape(-1)
    allowed = group_labels[:, None] == group_labels[None, :]
    grid = tokens.astype(jnp.float32).reshape(2, half_side, 2, half_side, D)
    hidden_one = modulate(grid, shift_one, scale_one).astype(jnp.bfloat16).reshape(tok_count, D)
    projected = jnp.dot(hidden_one, w_qkv, preferred_element_type=jnp.float32)

    def conv_queries(values, kernel):
        return depthwise(values.reshape(SIDE, SIDE, qkv_width), kernel, labels_grid)

    mixed_float, conv_pull = jax.vjp(conv_queries, projected, conv_qkv.astype(jnp.float32))
    mixed_qkv = mixed_float.astype(jnp.bfloat16)
    grouped = unshuffle(mixed_qkv.reshape(SIDE, SIDE, heads_dev, 3, HEAD_SIZE))
    attended, log_sums = lax.map(
        partial(group_forward, allowed=allowed, size_tag=size_tag), grouped
    )
    heads_out = shuffle(attended, SIDE).reshape(tok_count, heads_dev * HEAD_SIZE)
    attention = lax.psum(
        jnp.dot(heads_out, w_out, preferred_element_type=jnp.float32).astype(jnp.bfloat16), "tp"
    ).astype(jnp.float32)
    after_attention = grid + gate_one * attention.reshape(grid.shape)
    hidden_two = (
        modulate(after_attention, shift_two, scale_two).astype(jnp.bfloat16).reshape(tok_count, D)
    )
    upward = jnp.dot(hidden_two, w_up, preferred_element_type=jnp.float32)

    def activate(values, kernel):
        convolved = depthwise(values.reshape(SIDE, SIDE, hidden_width), kernel, labels_grid)
        return jax.nn.gelu(convolved, approximate=False).reshape(tok_count, hidden_width)

    act_float, act_pull = jax.vjp(activate, upward, conv_ffn.astype(jnp.float32))
    activation = act_float.astype(jnp.bfloat16)
    feed = lax.psum(
        jnp.dot(activation, w_down, preferred_element_type=jnp.float32).astype(jnp.bfloat16), "tp"
    ).astype(jnp.float32)
    result = after_attention + gate_two * feed.reshape(grid.shape)
    mixed = result.reshape(tok_count, D).astype(jnp.bfloat16)
    gradient_result = cotangent.astype(jnp.float32).reshape(grid.shape)
    grad_feed = (gate_two * gradient_result).astype(jnp.bfloat16).reshape(tok_count, D)
    grad_activation = jnp.dot(grad_feed, w_down.T, preferred_element_type=jnp.float32)
    grad_down_w = jnp.einsum("tf,td->fd", activation, grad_feed, preferred_element_type=jnp.float32)
    grad_upward, grad_kernel_ffn = act_pull(grad_activation)
    grad_up_low = grad_upward.astype(jnp.bfloat16)
    grad_up_w = jnp.einsum("td,tf->df", hidden_two, grad_up_low, preferred_element_type=jnp.float32)
    grad_hidden_two = lax.psum_scatter(
        jnp.dot(grad_up_low, w_up.T, preferred_element_type=jnp.float32).astype(jnp.bfloat16),
        "tp",
        scatter_dimension=0,
        tiled=True,
    ).astype(jnp.float32)
    quarter_rows = SIDE // tp_count
    quarter_tokens = tok_count // tp_count
    quarter_start = tp_rank * quarter_tokens
    quad_row = tp_rank * quarter_rows // half_side
    quarter_shape = (quarter_rows, 2, half_side, D)
    mods_quarter = lax.dynamic_index_in_dim(
        per_quad.reshape(2, 2, 6 * D), quad_row, 0, keepdims=False
    ).reshape(1, 2, 1, 6 * D)
    flat_after = after_attention.reshape(tok_count, D)
    after_quarter = lax.dynamic_slice_in_dim(flat_after, quarter_start, quarter_tokens, 0).reshape(
        quarter_shape
    )
    modulated_two, ln_pull_two = jax.vjp(
        modulate, after_quarter, mods_quarter[..., 3 * D : 4 * D], mods_quarter[..., 4 * D : 5 * D]
    )
    grad_after_ln, grad_shift_two, grad_scale_two = ln_pull_two(
        grad_hidden_two.reshape(quarter_shape)
    )
    grad_ln_rows = lax.all_gather(
        grad_after_ln.reshape(quarter_tokens, D).astype(jnp.bfloat16), "tp", axis=0, tiled=True
    ).astype(jnp.float32)
    flat_grad_result = gradient_result.reshape(tok_count, D)
    grad_after = flat_grad_result + grad_ln_rows
    feed_quarter = lax.dynamic_slice_in_dim(feed, quarter_start, quarter_tokens, 0).reshape(
        quarter_shape
    )
    result_grad_quarter = lax.dynamic_slice_in_dim(
        flat_grad_result, quarter_start, quarter_tokens, 0
    ).reshape(quarter_shape)
    grad_gate_two = jnp.sum(result_grad_quarter * feed_quarter, axis=(0, 2))
    grad_attention = (
        (gate_one * grad_after.reshape(grid.shape)).astype(jnp.bfloat16).reshape(tok_count, D)
    )
    grad_heads = jnp.dot(grad_attention, w_out.T, preferred_element_type=jnp.float32).astype(
        jnp.bfloat16
    )
    grad_out_w = jnp.einsum(
        "tc,td->cd", heads_out, grad_attention, preferred_element_type=jnp.float32
    )
    after_grad_quarter = lax.dynamic_slice_in_dim(grad_after, quarter_start, quarter_tokens, 0)
    attention_quarter = lax.dynamic_slice_in_dim(attention, quarter_start, quarter_tokens, 0)
    grad_gate_one = jnp.sum(
        (after_grad_quarter * attention_quarter).reshape(quarter_shape), axis=(0, 2)
    )
    grad_grouped = unshuffle(grad_heads.reshape(SIDE, SIDE, heads_dev, HEAD_SIZE))
    grad_qkv_groups = lax.map(
        partial(group_backward, allowed=allowed, size_tag=size_tag),
        (grouped, grad_grouped, log_sums),
    )
    grad_mixed = shuffle(grad_qkv_groups, SIDE).reshape(SIDE, SIDE, qkv_width)
    grad_projected, grad_kernel_qkv = conv_pull(grad_mixed)
    grad_proj_low = grad_projected.astype(jnp.bfloat16)
    grad_qkv_w = jnp.einsum(
        "td,tc->dc", hidden_one, grad_proj_low, preferred_element_type=jnp.float32
    )
    grad_hidden_one = lax.psum_scatter(
        jnp.dot(grad_proj_low, w_qkv.T, preferred_element_type=jnp.float32).astype(jnp.bfloat16),
        "tp",
        scatter_dimension=0,
        tiled=True,
    ).astype(jnp.float32)
    tokens_quarter = lax.dynamic_slice_in_dim(
        grid.reshape(tok_count, D), quarter_start, quarter_tokens, 0
    ).reshape(quarter_shape)
    modulated_one, ln_pull_one = jax.vjp(
        modulate, tokens_quarter, mods_quarter[..., 0:D], mods_quarter[..., D : 2 * D]
    )
    grad_tokens_ln, grad_shift_one, grad_scale_one = ln_pull_one(
        grad_hidden_one.reshape(quarter_shape)
    )
    grad_tokens = after_grad_quarter + grad_tokens_ln.reshape(quarter_tokens, D)
    quad_rows = jnp.concatenate(
        [
            grad_shift_one.reshape(2, D),
            grad_scale_one.reshape(2, D),
            grad_gate_one,
            grad_shift_two.reshape(2, D),
            grad_scale_two.reshape(2, D),
            grad_gate_two,
        ],
        axis=-1,
    )
    row_pick = (lax.iota(jnp.int32, 2) == quad_row)[:, None, None]
    grad_quads = jnp.where(row_pick, quad_rows[None], jnp.zeros_like(quad_rows[None])).reshape(
        4, 6 * D
    )
    merged_slot = jnp.concatenate(
        [jnp.sum(grad_quads, axis=0, keepdims=True), jnp.zeros((SLOTS - 1, 6 * D), jnp.float32)],
        axis=0,
    )
    grad_slots = jnp.where(size_tag == 1, merged_slot, grad_quads)
    grad_mod_cols = lax.psum_scatter(
        grad_slots.astype(jnp.bfloat16), "tp", scatter_dimension=1, tiled=True
    ).astype(jnp.float32)
    grad_mod_w = jnp.dot(
        activated.astype(jnp.float32).T, grad_mod_cols, precision=lax.Precision.HIGHEST
    )
    grad_activated = jnp.dot(
        grad_mod_cols, w_mod.astype(jnp.float32).T, precision=lax.Precision.HIGHEST
    )
    silu_value, silu_pull = jax.vjp(jax.nn.silu, condition)
    grad_cond_part = silu_pull(grad_activated)[0]
    grad_condition = lax.psum(grad_cond_part, "tp")
    grad_cols = lax.all_to_all(grad_condition, "dp", split_axis=1, concat_axis=0, tiled=True)
    time_iota = lax.broadcasted_iota(jnp.int32, (time_index.shape[0], time_table.shape[0]), 1)
    time_hits = (time_index[:, None] == time_iota).astype(jnp.float32)
    grad_time = jnp.dot(time_hits.T, grad_cols, precision=lax.Precision.HIGHEST)
    class_iota = lax.broadcasted_iota(jnp.int32, (class_index.shape[0], class_table.shape[0]), 1)
    class_hits = (class_index[:, None] == class_iota).astype(jnp.float32)
    grad_class = jnp.dot(class_hits.T, grad_cols, precision=lax.Precision.HIGHEST)
    summed_qkv, summed_conv_qkv, summed_out, summed_mod, summed_up, summed_conv_ffn, summed_down = (
        lax.psum_scatter(grad_qkv_w, "dp", scatter_dimension=0, tiled=True),
        lax.psum_scatter(grad_kernel_qkv, "dp", scatter_dimension=1, tiled=True),
        lax.psum_scatter(grad_out_w, "dp", scatter_dimension=1, tiled=True),
        lax.psum_scatter(grad_mod_w, "dp", scatter_dimension=0, tiled=True),
        lax.psum_scatter(grad_up_w, "dp", scatter_dimension=0, tiled=True),
        lax.psum_scatter(grad_kernel_ffn, "dp", scatter_dimension=1, tiled=True),
        lax.psum_scatter(grad_down_w, "dp", scatter_dimension=1, tiled=True),
    )
    return (
        mixed,
        grad_tokens,
        grad_time,
        grad_class,
        summed_mod,
        summed_qkv,
        summed_conv_qkv,
        summed_out,
        summed_up,
        summed_conv_ffn,
        summed_down,
    )


def solution(mesh):
    in_specs = (
        P("dp", None),
        P("dp", None),
        P("dp"),
        P(),
        P(),
        P(),
        P(),
        P(None, "tp"),
        P(None, "tp"),
        P(None, "tp"),
        P("tp", None),
        P(None, "tp"),
        P(None, "tp"),
        P("tp", None),
    )
    out_specs = (
        P("dp", None),
        P(("dp", "tp"), None),
        P(None, "dp"),
        P(None, "dp"),
        P("dp", "tp"),
        P("dp", "tp"),
        P(None, ("tp", "dp")),
        P("tp", "dp"),
        P("dp", "tp"),
        P(None, ("tp", "dp")),
        P("tp", "dp"),
    )
    return jax.shard_map(
        per_device, mesh=mesh, in_specs=in_specs, out_specs=out_specs, check_vma=False
    )
```

profile of v0, /device:TPU:0, one launch (start us, length us, event | category | flops | bytes accessed | tf_op | source)
XLA Modules:
  0.0 1967.9 jit_solution(16814510556548511663)
XLA Ops:
  22.4 15.0 all_gather.6
  53.2 39.4 %add_convert_fusion = bf16[64,64,576]{2,1,0:T(8,128)(2,1)} fusion(f32[64,64,576]{2,1,0:T(8,128)} %fusion.67, f32[576]{0:T(1024)S(1)} %get-tuple-element.161, f32[576]{0:T(1024)S(1)} %copy-done.55, f32[576]{0:T(1024)S(1)} %copy-done.57, f32[576]{0:T(1024)S(1)} %copy-done.59, f32[576]{0:T(1024)S(1)} %copy-done.61, f32[576]{0:T(1024)S(1)} %copy-done.63, ...), kind=kLoop, calls=%fused_computation.168 | loop fusion | flops 61341696 | bytes 14209280 | tf_op jit(solution)/shard_map/convert_element_type | solution.py:183
  92.7 23.2 %reshape_reshape.12 = bf16[32,2,32,2,3,3,64]{6,5,4,3,2,1,0:T(4,128)(2,1)} reshape(bf16[64,64,576]{2,1,0:T(8,128)(2,1)} %add_convert_fusion) | data formatting | bytes 9437184 | tf_op jit(solution)/shard_map/reshape;reshape | solution.py:49
  136.3 91.1 %while.24 = (s32[]{:T(128)}, bf16[4,1024,3,64]{1,3,2,0:T(8,128)(2,1)S(1)}, f32[4,1024,3]{1,2,0:T(4,128)}, bf16[4,1024,3,3,64]{1,4,2,3,0:T(8,128)(2,1)}, s32[1024]{0:T(1024)S(1)}, /*index=5*/s32[]{:T(128)}) while((s32[]{:T(128)}, bf16[4,1024,3,64]{1,3,2,0:T(8,128)(2,1)S(1)}, f32[4,1024,3]{1,2,0:T(4,128)}, ...), condition=%wide.region_5.7_spmd.clone, body=%wide.region_2.6_spmd.clone.sunk | while | flops 844297216 | bytes 45989976 | solution.py:185
  252.0 224.0 %all-reduce.44.cloned.1.call-done = bf16[4096,768]{1,0:T(8,128)(2,1)} async-done(((bf16[4096,768]{1,0:T(8,128)(2,1)}), bf16[4096,768]{1,0:T(8,128)(2,1)}) %all-reduce.44.cloned.1.call-update) | async-done | bytes 6291472 | tf_op jit(solution)/shard_map/psum | solution.py:189
  476.0 11.2 fusion.101
  508.8 57.6 %multiply_convert_fusion.1 = (bf16[64,64,768]{2,1,0:T(8,128)(2,1)S(1)}, f32[64,64,768]{2,1,0:T(8,128)}, f32[64,64,768]{2,1,0:T(8,128)}) fusion(pred[64,64]{1,0:T(8,128)(4,1)S(1)} %copy-done.33, f32[768]{0:T(1024)S(1)} %get-tuple-element.152, pred[64,64]{1,0:T(8,128)(4,1)S(1)} %copy-done.15, f32[768]{0:T(1024)S(1)} %get-tuple-element.153, ...), kind=kLoop, calls=%fused_computation.118 | loop fusion | flops 283115520 | bytes 44100608 | tf_op jit(solution)/shard_map/convert_element_type | solution.py:203
  576.1 221.8 %all-reduce.46.cloned.1.call-done = bf16[4096,768]{1,0:T(8,128)(2,1)} async-done(((bf16[4096,768]{1,0:T(8,128)(2,1)}), bf16[4096,768]{1,0:T(8,128)(2,1)}) %all-reduce.46.cloned.1.call-update) | async-done | bytes 6291472 | tf_op jit(solution)/shard_map/psum | solution.py:204
  798.0 14.7 fusion.46
  812.6 70.9 %multiply_reduce_fusion.9 = (f32[768]{0:T(1024)}, f32[768]{0:T(1024)}, f32[768]{0:T(1024)}, f32[768]{0:T(1024)}, f32[768]{0:T(1024)}, /*index=5*/f32[768]{0:T(10...) fusion(f32[64,64,768]{2,1,0:T(8,128)} %fusion.65, ...), kind=kOutput, calls=%fused_computation.107 | convolution fusion | flops 4960803840 | bytes 70449152 | tf_op jit(solution)/shard_map/dot_general | solution.py:211
  883.6 32.2 %multiply_select_fusion.8 = (f32[64,64,768]{2,1,0:T(8,128)S(1)}, f32[64,64,768]{2,1,0:T(8,128)}, f32[64,64,768]{2,1,0:T(8,128)}, f32[64,64,768]{2,1,0:T(8,128)},...) fusion(f32[64,64,768]{2,1,0:T(8,128)} %get-tuple-element.254, ...), kind=kLoop, calls=%fused_computation.116 | loop fusion | flops 47185920 | bytes 113299456 | tf_op jit(solution)/shard_map/transpose(jvp(jit(_where)))/select_n | solution.py:40
  915.7 19.0 pad_add_fusion
  934.8 29.6 %fusion.47 = bf16[64,64,768]{2,1,0:T(8,128)(2,1)} fusion(f32[64,64,768]{2,1,0:T(8,128)} %get-tuple-element.210, f32[64,64,768]{2,1,0:T(8,128)} %get-tuple-element.216, f32[64,64,768]{2,1,0:T(8,128)} %get-tuple-element.217, f32[64,64,768]{2,1,0:T(8,128)} %get-tuple-element.218, f32[64,64,768]{2,1,0:T(8,128)} %get-tuple-element.219, f32[66,66,768]{2,1,0:T(8,128)} %pad_add_fusion), kind=kLoop, calls=%fused_computation.88 | loop fusion | flops 18874368 | bytes 81788928 | tf_op jit(solution)/shard_map/convert.1
  979.0 105.3 %reduce-scatter.17.cloned.1.call-done = bf16[1024,768]{1,0:T(8,128)(2,1)} async-done(((bf16[4096,768]{1,0:T(8,128)(2,1)}), bf16[1024,768]{1,0:T(8,128)(2,1)}) %reduce-scatter.17.cloned.1.call-update) | async-done | bytes 1572880 | tf_op jit(solution)/shard_map/reduce_scatter | solution.py:216
  1092.3 115.9 %all-gather.2.cloned.1.call-done = bf16[4096,768]{1,0:T(8,128)(2,1)} async-done(((bf16[1024,768]{1,0:T(8,128)(2,1)}), bf16[4096,768]{1,0:T(8,128)(2,1)}) %all-gather.2.cloned.1.call-update) | async-done | bytes 6291472 | tf_op jit(solution)/shard_map/all_gather | solution.py:240
  1208.2 10.9 fusion.43
  1246.3 109.3 %while.25 = (s32[]{:T(128)}, f32[4,1024,3,3,64]{1,4,2,3,0:T(8,128)}, bf16[4,1024,3,3,64]{1,4,2,3,0:T(8,128)(2,1)}, f32[4,1024,3]{1,2,0:T(4,128)}, bf16[4,1024,3,...) while((s32[]{:T(128)}, f32[4,1024,3,3,64]{1,4,2,3,0:T(8,128)}, ...), condition=%wide.region_17.19_spmd.clone, body=%wide.region_15.18_spmd.clone.sunk | while | flops 2063070208 | bytes 117145728 | solution.py:267
  1355.6 13.8 copy.59
  1369.4 26.1 %copy.60 = f32[32,2,32,2,3,3,64]{6,5,4,3,2,1,0:T(4,128)} copy(f32[32,2,32,2,3,3,64]{6,2,0,5,4,3,1:T(8,128)} %bitcast.260) | data formatting | bytes 18874368 | tf_op jit(solution)/shard_map/transpose | solution.py:59
  1395.5 26.3 %reshape_reshape.15 = f32[64,64,576]{2,1,0:T(8,128)} reshape(f32[32,2,32,2,3,3,64]{6,5,4,3,2,1,0:T(4,128)} %copy.60) | data formatting | bytes 18874368 | tf_op jit(solution)/shard_map/reshape;reshape | solution.py:271
  1422.0 43.9 %multiply_reduce_fusion.20 = (f32[576]{0:T(1024)S(1)}, f32[576]{0:T(1024)S(1)}, f32[576]{0:T(1024)S(1)}, f32[576]{0:T(1024)S(1)}, f32[576]{0:T(1024)S(1)}, /*ind...) fusion(f32[64,64,576]{2,1,0:T(8,128)} %reshape_reshape.15, ...), kind=kLoop, calls=%fused_computation.159 | loop fusion | flops 66055104 | bytes 28367360 | tf_op jit(solution)/shard_map/transpose(jvp())/reduce_sum | solution.py:40
  1465.9 29.3 %multiply_select_fusion.16 = (f32[64,64,576]{2,1,0:T(8,128)}, f32[64,64,576]{2,1,0:T(8,128)}, f32[64,64,576]{2,1,0:T(8,128)}, f32[64,64,576]{2,1,0:T(8,128)}, f3...) fusion(f32[64,64,576]{2,1,0:T(8,128)} %reshape_reshape.15, ...), kind=kLoop, calls=%fused_computation.167 | loop fusion | flops 35389440 | bytes 84981760 | tf_op jit(solution)/shard_map/transpose(jvp(jit(_where)))/select_n | solution.py:40
  1495.3 14.7 pad_add_fusion.6
  1509.9 20.1 %fusion.63 = bf16[64,64,576]{2,1,0:T(8,128)(2,1)} fusion(f32[64,64,576]{2,1,0:T(8,128)} %get-tuple-element.223, f32[64,64,576]{2,1,0:T(8,128)} %get-tuple-element.225, f32[64,64,576]{2,1,0:T(8,128)} %get-tuple-element.226, f32[64,64,576]{2,1,0:T(8,128)} %get-tuple-element.227, f32[64,64,576]{2,1,0:T(8,128)} %get-tuple-element.228, ...), kind=kLoop, calls=%fused_computation.146 | loop fusion | flops 14155776 | bytes 61341696 | tf_op jit(solution)/shard_map/convert
  1582.5 66.1 %reduce-scatter.19.cloned.1.call-done = bf16[1024,768]{1,0:T(8,128)(2,1)} async-done(((bf16[4096,768]{1,0:T(8,128)(2,1)}), bf16[1024,768]{1,0:T(8,128)(2,1)}) %reduce-scatter.19.cloned.1.call-update) | async-done | bytes 1572880 | tf_op jit(solution)/shard_map/reduce_scatter | solution.py:277
  1711.3 22.8 %reduce-scatter.33.cloned.1.call-done = f32[96,9]{1,0:T(8,128)} async-done(((f32[768,9]{1,0:T(8,128)}), f32[96,9]{1,0:T(8,128)}) %reduce-scatter.33.cloned.1.call-update) | async-done | bytes 3472
  1735.6 22.9 %all-reduce.40 = f32[9,576]{1,0:T(8,128)S(1)} all-reduce(f32[9,576]{1,0:T(8,128)S(1)} %pad_add_fusion.13), channel_id=7, replica_groups=mesh['dp'=8,'tp'=4] {'dp'}, use_global_device_ids=true, to_apply=%region_43.45.clone | all-reduce | flops 5184 | bytes 41472
  1760.2 19.3 psum.23
  1789.8 28.6 %reduce-scatter.27.cloned.1.call-done = f32[768,96]{0,1:T(8,128)} async-done(((f32[768,768]{0,1:T(8,128)}), f32[768,96]{0,1:T(8,128)}) %reduce-scatter.27.cloned.1.call-update) | async-done | bytes 294928 | tf_op jit(solution)/shard_map/reduce_scatter | solution.py:339
  1818.4 46.1 %reduce-scatter.25.cloned.1.call-done = f32[96,768]{1,0:T(8,128)} async-done(((f32[768,768]{1,0:T(8,128)}), f32[96,768]{1,0:T(8,128)}) %reduce-scatter.25.cloned.1.call-update) | async-done | bytes 294928 | tf_op jit(solution)/shard_map/reduce_scatter | solution.py:337
  1864.6 44.2 %reduce-scatter.23.cloned.1.call-done = f32[96,576]{1,0:T(8,128)} async-done(((f32[768,576]{1,0:T(8,128)}), f32[96,576]{1,0:T(8,128)}) %reduce-scatter.23.cloned.1.call-update) | async-done | bytes 221200 | tf_op jit(solution)/shard_map/reduce_scatter | solution.py:333
  1908.8 51.9 %reduce-scatter.21.cloned.1.call-done = f32[96,1152]{1,0:T(8,128)} async-done(((f32[768,1152]{1,0:T(8,128)}), f32[96,1152]{1,0:T(8,128)}) %reduce-scatter.21.cloned.1.call-update) | async-done | bytes 442384 | tf_op jit(solution)/shard_map/reduce_scatter | solution.py:336
  (420 shorter events, 482.6 us)
Async XLA Ops:
  7.2 468.7 %all-reduce.44.cloned.1.call-start = ((), (), s32[]{:S(2)}) async-start(), calls=%async_computation.10 | async-start | bytes 12582912 | tf_op jit(solution)/shard_map/psum | solution.py:189
  17.0 36.1 %copy-start.23 = (pred[64,64]{1,0:T(8,128)(4,1)}, pred[64,64]{1,0:T(8,128)(4,1)S(1)}, u32[]{:S(2)}) copy-start(pred[64,64]{1,0:T(8,128)(4,1)S(1)} %get-tuple-element.244) | copy-start | bytes 12292
  17.0 36.1 %copy-start.26 = (pred[64,64]{1,0:T(8,128)(4,1)}, pred[64,64]{1,0:T(8,128)(4,1)S(1)}, u32[]{:S(2)}) copy-start(pred[64,64]{1,0:T(8,128)(4,1)S(1)} %get-tuple-element.245) | copy-start | bytes 12292
  245.7 230.3 %copy-start.41 = (f32[2,2,768]{2,1,0:T(2,128)S(1)}, f32[2,2,768]{2,1,0:T(2,128)}, u32[]{:S(2)}) copy-start(f32[2,2,768]{2,1,0:T(2,128)} %get-tuple-element.237) | copy-start | bytes 36868
  251.8 546.1 %all-reduce.46.cloned.1.call-start = ((), (), s32[]{:S(2)}) async-start(), calls=%async_computation.11 | async-start | bytes 12582912 | tf_op jit(solution)/shard_map/psum | solution.py:204
  508.8 60.2 %copy-start.90 = (bf16[768,768]{1,0:T(8,128)(2,1)S(1)}, bf16[768,768]{1,0:T(8,128)(2,1)}, u32[]{:S(2)}) copy-start(bf16[768,768]{1,0:T(8,128)(2,1)} %param.33) | copy-start | bytes 3538948
  569.0 228.9 %copy-start.50 = (f32[2,2,768]{2,1,0:T(2,128)S(1)}, f32[2,2,768]{2,1,0:T(2,128)}, u32[]{:S(2)}) copy-start(f32[2,2,768]{2,1,0:T(2,128)} %get-tuple-element.234) | copy-start | bytes 36868
  576.1 508.2 %reduce-scatter.17.cloned.1.call-start = ((), (), s32[]{:S(2)}) async-start(), calls=%async_computation.12 | async-start | bytes 7864320 | tf_op jit(solution)/shard_map/reduce_scatter | solution.py:216
  974.4 233.7 %all-gather.2.cloned.1.call-start = ((), (), s32[]{:S(2)}) async-start(), calls=%async_computation.13 | async-start | bytes 7864320 | tf_op jit(solution)/shard_map/all_gather | solution.py:240
  979.0 229.2 %copy-start.42 = (f32[2,2,768]{2,1,0:T(2,128)S(1)}, f32[2,2,768]{2,1,0:T(2,128)}, u32[]{:S(2)}) copy-start(f32[2,2,768]{2,1,0:T(2,128)} %get-tuple-element.237) | copy-start | bytes 36868
  979.0 113.3 %copy-start.48 = (f32[1024]{0:T(1024)}, f32[1024]{0:T(1024)S(1)}, u32[]{:S(2)}) copy-start(f32[1024]{0:T(1024)S(1)} %broadcast_multiply_fusion.5) | copy-start | bytes 12292
  1092.2 556.4 %reduce-scatter.19.cloned.1.call-start = ((), (), s32[]{:S(2)}) async-start(), calls=%async_computation.14 | async-start | bytes 7864320 | tf_op jit(solution)/shard_map/reduce_scatter | solution.py:277
  1092.2 129.5 %copy-start.36 = (bf16[192,768]{1,0:T(8,128)(2,1)S(1)}, bf16[192,768]{1,0:T(8,128)(2,1)}, u32[]{:S(2)}) copy-start(bf16[192,768]{1,0:T(8,128)(2,1)} %param.30) | copy-start | bytes 884740
  1421.9 44.0 %copy-start.54 = (f32[576]{0:T(1024)S(1)}, f32[576]{0:T(1024)}, u32[]{:S(2)}) copy-start(f32[576]{0:T(1024)} %copy-done.53) | copy-start | bytes 6916
  1421.9 44.0 %copy-start.56 = (f32[576]{0:T(1024)S(1)}, f32[576]{0:T(1024)}, u32[]{:S(2)}) copy-start(f32[576]{0:T(1024)} %get-tuple-element.162) | copy-start | bytes 6916
  1421.9 44.0 %copy-start.58 = (f32[576]{0:T(1024)S(1)}, f32[576]{0:T(1024)}, u32[]{:S(2)}) copy-start(f32[576]{0:T(1024)} %get-tuple-element.163) | copy-start | bytes 6916
  1421.9 44.0 %copy-start.60 = (f32[576]{0:T(1024)S(1)}, f32[576]{0:T(1024)}, u32[]{:S(2)}) copy-start(f32[576]{0:T(1024)} %get-tuple-element.164) | copy-start | bytes 6916
  1421.9 44.0 %copy-start.62 = (f32[576]{0:T(1024)S(1)}, f32[576]{0:T(1024)}, u32[]{:S(2)}) copy-start(f32[576]{0:T(1024)} %get-tuple-element.165) | copy-start | bytes 6916
  1421.9 44.0 %copy-start.64 = (f32[576]{0:T(1024)S(1)}, f32[576]{0:T(1024)}, u32[]{:S(2)}) copy-start(f32[576]{0:T(1024)} %get-tuple-element.166) | copy-start | bytes 6916
  1422.0 44.0 %copy-start.66 = (f32[576]{0:T(1024)S(1)}, f32[576]{0:T(1024)}, u32[]{:S(2)}) copy-start(f32[576]{0:T(1024)} %get-tuple-element.167) | copy-start | bytes 6916
  1422.0 44.0 %copy-start.68 = (f32[576]{0:T(1024)S(1)}, f32[576]{0:T(1024)}, u32[]{:S(2)}) copy-start(f32[576]{0:T(1024)} %get-tuple-element.168) | copy-start | bytes 6916
  1539.4 167.0 %reduce-scatter.29.cloned.1.call-start = ((), (), s32[]{:S(2)}) async-start(), calls=%async_computation.19 | async-start | bytes 1474560
  1573.3 75.2 %copy-start.43 = (f32[2,768]{1,0:T(2,128)S(1)}, f32[2,768]{1,0:T(2,128)}, u32[]{:S(2)}) copy-start(f32[2,768]{1,0:T(2,128)} %get-tuple-element.238) | copy-start | bytes 18436
  1667.9 66.1 %reduce-scatter.33.cloned.1.call-start = ((), (), s32[]{:S(2)}) async-start(), calls=%async_computation.21 | async-start | bytes 442368
  1668.9 114.6 %reduce-scatter.31.cloned.1.call-start = ((), (), s32[]{:S(2)}) async-start(), calls=%async_computation.20 | async-start | bytes 884736
  1675.9 142.6 %reduce-scatter.27.cloned.1.call-start = ((), (), s32[]{:S(2)}) async-start(), calls=%async_computation.18 | async-start | bytes 2654208 | tf_op jit(solution)/shard_map/reduce_scatter | solution.py:339
  1686.3 178.3 %reduce-scatter.25.cloned.1.call-start = ((), (), s32[]{:S(2)}) async-start(), calls=%async_computation.17 | async-start | bytes 2654208 | tf_op jit(solution)/shard_map/reduce_scatter | solution.py:337
  1696.6 212.2 %reduce-scatter.23.cloned.1.call-start = ((), (), s32[]{:S(2)}) async-start(), calls=%async_computation.16 | async-start | bytes 2211840 | tf_op jit(solution)/shard_map/reduce_scatter | solution.py:333
  1706.3 81.2 %copy-start.88 = (s32[32]{0:T(128)S(1)}, s32[32]{0:T(128)}, u32[]{:S(2)}) copy-start(s32[32]{0:T(128)} %param.24) | copy-start | bytes 388
  1706.4 82.3 %copy-start.89 = (s32[32]{0:T(128)S(1)}, s32[32]{0:T(128)}, u32[]{:S(2)}) copy-start(s32[32]{0:T(128)} %param.23) | copy-start | bytes 388
  1706.4 254.3 %reduce-scatter.21.cloned.1.call-start = ((), (), s32[]{:S(2)}) async-start(), calls=%async_computation.15 | async-start | bytes 3981312 | tf_op jit(solution)/shard_map/reduce_scatter | solution.py:336
  1779.5 8.0 all-to-all-start
  (80 other events, 1098.6 us)
Sparse Core Ops, SparseCore 0:
  251.9 223.9 all-reduce.43
  576.2 221.7 all-reduce.45
  974.5 109.6 reduce-scatter.16
  1092.3 115.8 all-gather.1
  1539.6 108.9 reduce-scatter.18
  1668.0 29.8 reduce-scatter.28
  1701.5 32.4 reduce-scatter.32
  1737.2 34.9 reduce-scatter.30
  1776.1 42.3 reduce-scatter.26
  1822.2 42.3 reduce-scatter.24
  1868.6 40.1 reduce-scatter.22
  1912.7 47.9 reduce-scatter.20
where the time goes:
time: 1980 us; the launch traced here: 1970 us
  waiting for transfers between devices  929 us (47%)
  other arithmetic  493 us (25%)
  matrix products  281 us (14%)
  local copies, waits for them, and re-layouts  184 us (9%)
  blocking collectives  57.2 us (3%)
    psum x1, waiting for transfers between devices, per_device(): lax.psum(jnp.dot(heads_out, w_out, preferred_element_type=jnp.float32).as...  224 us
    psum x1, waiting for transfers between devices, per_device(): lax.psum(jnp.dot(activation, w_down, preferred_element_type=jnp.float32)....  222 us
    all_gather x1, waiting for transfers between devices, per_device(): lax.all_gather(grad_after_ln.reshape(quarter_tokens, D).astype(jnp.bfloat...  116 us
    reduce_scatter x1, waiting for transfers between devices, per_device(): lax.psum_scatter(jnp.dot(grad_up_low, w_up.T, preferred_element_type=jnp....  105 us
    dot_general x1, matrix products, per_device(): jnp.dot(grad_feed, w_down.T, preferred_element_type=jnp.float32)  70.9 us
    reduce_scatter x1, waiting for transfers between devices, per_device(): lax.psum_scatter(jnp.dot(grad_proj_low, w_qkv.T, preferred_element_type=j...  66.1 us
    select_n x2, other arithmetic, depthwise(): jnp.where(same_item[:, :, None], moved, jnp.zeros_like(moved))  61.5 us
    convert_element_type x1, other arithmetic, per_device(): activation = act_float.astype(jnp.bfloat16)  57.6 us
  transfers between devices with their start and end apart: 13, of which 11 were waited for; matrix products, arithmetic and copies ran while one was open for 5% of the time, Pallas kernels for 0%

commit v1 on v0

v1 whole, which is shorter than its diff:
```python
from functools import partial

import jax
import jax.numpy as jnp
import numpy as np
from jax import lax
from jax.experimental import pallas as pl
from jax.experimental.pallas import tpu as pltpu
from jax.sharding import PartitionSpec as P

D = 768
HEAD_SIZE = 64
SIDE = 64
SLOTS = 4
TOK = SIDE * SIDE
HALO = 2
QROWS = 16
QTOK = QROWS * SIDE
XTOK = (QROWS + 2 * HALO) * SIDE
F32 = jnp.float32
BF16 = jnp.bfloat16
VMEM_MAX = 66_000_000


def dot_nn(a, b):
    return lax.dot_general(a, b, (((1,), (0,)), ((), ())), preferred_element_type=F32)


def dot_nt(a, b):
    return lax.dot_general(a, b, (((1,), (1,)), ((), ())), preferred_element_type=F32)


def dot_tn(a, b):
    return lax.dot_general(a, b, (((0,), (0,)), ((), ())), preferred_element_type=F32)


def parity_matrix():
    one = np.zeros((SIDE, SIDE), np.float32)
    for parity in range(2):
        for j in range(SIDE // 2):
            one[parity * 32 + j, 2 * j + parity] = 1.0
    return jnp.asarray(np.kron(np.eye(4, dtype=np.float32), one), BF16)


def normalised(values):
    mean = jnp.mean(values, axis=-1, keepdims=True)
    centred = values - mean
    variance = jnp.mean(centred * centred, axis=-1, keepdims=True)
    rstd = lax.rsqrt(variance + 1e-06)
    return centred * rstd, rstd


def by_half(values, part):
    rows = values.shape[0]
    shaped = values.reshape(rows // 32, 2, 16, values.shape[-1])
    return (shaped * part[None, :, None, :]).reshape(values.shape)


def spread(part, rows):
    width = part.shape[-1]
    full = jnp.broadcast_to(part[None, :, None, :], (rows // 32, 2, 16, width))
    return full.reshape(rows, width)


def half_sums(values):
    return jnp.sum(values.reshape(values.shape[0] // 32, 2, 16, values.shape[-1]), axis=0)


def column_masks(tag, width):
    j = lax.broadcasted_iota(jnp.int32, (32, width), 0)
    split = tag == 0
    left = jnp.where((j == 0) | ((j == 16) & split), 0.0, 1.0)
    right = jnp.where((j == 31) | ((j == 15) & split), 0.0, 1.0)
    return left, right


def row_scales(tag, row):
    inside = (row >= 0) & (row < SIDE)
    down = jnp.where(inside & jnp.logical_not((tag == 0) & (row == 31)), 1.0, 0.0)
    up = jnp.where(inside & jnp.logical_not((tag == 0) & (row == 32)), 1.0, 0.0)
    return down, up


def conv_step(even, odd, masks, taps, down, up, carry):
    left, right = masks
    odd_left = pltpu.roll(odd, 1, 0) * left
    even_right = pltpu.roll(even, 31, 0) * right
    before_e, before_o, here_e, here_o = carry

    def terms(k):
        return (
            k[0] * odd_left + k[1] * even + k[2] * odd,
            k[0] * even + k[1] * odd + k[2] * even_right,
        )

    last = [t * up for t in taps[6:9]]
    middle = taps[3:6]
    first = [t * down for t in taps[0:3]]
    last_e, last_o = terms(last)
    mid_e, mid_o = terms(middle)
    first_e, first_o = terms(first)
    done = (before_e + last_e, before_o + last_o)
    return done, (here_e + mid_e, here_o + mid_o, first_e, first_o), (odd_left, even_right)


def no_carry(width):
    zero = jnp.zeros((32, width), F32)
    return (zero, zero, zero, zero)


def first_kernel(tag_ref, tok_ref, shift_ref, scale_ref, w_ref, taps_ref, perm_ref, hid_ref, proj_ref, mix_ref, field):
    step = pl.program_id(0)
    tag = tag_ref[0]
    width = w_ref.shape[1]

    @pl.when(step == 0)
    def _():
        field[pl.ds(0, SIDE), :] = jnp.zeros((SIDE, width), F32)
        field[pl.ds((SIDE + 1) * SIDE, SIDE), :] = jnp.zeros((SIDE, width), F32)

    @pl.when(step < 4)
    def _():
        half = step // 2
        shift = shift_ref[half]
        scale = 1.0 + scale_ref[half]

        def chunk(i, carry):
            rows = pl.ds(pl.multiple_of(i * 256, 256), 256)
            ordered = dot_nn(perm_ref[...], tok_ref[rows, :])
            unit, _ = normalised(ordered)
            hidden = (by_half(unit, scale) + spread(shift, 256)).astype(BF16)
            hid_ref[rows, :] = hidden
            out = dot_nn(hidden, w_ref[...])
            proj_ref[rows, :] = out
            field[pl.ds(pl.multiple_of((step * 16 + 1) * SIDE + i * 256, 64), 256), :] = out
            return carry

        lax.fori_loop(0, 4, chunk, 0)

    @pl.when(step > 0)
    def _():
        base = (step - 1) * 16 - 1
        for lane in range(0, width, 128):
            size = min(128, width - lane)
            lanes = slice(lane, lane + size)
            masks = column_masks(tag, size)
            taps = [taps_ref[t : t + 1, lanes] for t in range(9)]

            def one(n, carry):
                row = base + n
                start = pl.multiple_of((row + 1) * SIDE, SIDE)
                even = field[pl.ds(start, 32), lanes]
                odd = field[pl.ds(start + 32, 32), lanes]
                down, up = row_scales(tag, row)
                done, carry, _ = conv_step(even, odd, masks, taps, down, up, carry)
                return done, carry

            def loop(n, carry):
                done, carry = one(n, carry)
                start = pl.multiple_of((n - 2) * SIDE, SIDE)
                mix_ref[pl.ds(start, 32), lanes] = done[0].astype(BF16)
                mix_ref[pl.ds(start + 32, 32), lanes] = done[1].astype(BF16)
                return carry

            _, carry = one(0, no_carry(size))
            _, carry = one(1, carry)
            lax.fori_loop(2, 18, loop, carry)


def first_stage(tag, tokens, shift, scale, w_qkv, taps, perm):
    width = w_qkv.shape[1]
    whole = lambda shape: pl.BlockSpec(shape, lambda s: (0,) * len(shape))
    ahead = lambda w: pl.BlockSpec((1024, w), lambda s: (jnp.minimum(s, 3), 0))
    return pl.pallas_call(
        first_kernel,
        grid=(5,),
        in_specs=[
            pl.BlockSpec(memory_space=pltpu.SMEM),
            ahead(D),
            whole((2, 2, D)),
            whole((2, 2, D)),
            whole((D, width)),
            whole((9, width)),
            whole((256, 256)),
        ],
        out_specs=[
            ahead(D),
            ahead(width),
            pl.BlockSpec((1024, width), lambda s: (jnp.maximum(s - 1, 0), 0)),
        ],
        out_shape=[
            jax.ShapeDtypeStruct((TOK, D), BF16),
            jax.ShapeDtypeStruct((TOK, width), F32),
            jax.ShapeDtypeStruct((TOK, width), BF16),
        ],
        scratch_shapes=[pltpu.VMEM(((SIDE + 2) * SIDE, width), F32)],
        compiler_params=pltpu.CompilerParams(vmem_limit_bytes=VMEM_MAX),
        name="first_stage",
    )(tag, tokens, shift, scale, w_qkv, taps, perm)


def to_row(column, count):
    return jnp.transpose(jnp.broadcast_to(column, (count, 128)))[0:1, :]


def attend_kernel(tag_ref, x_ref, o_ref, lse_ref, *, heads):
    tag = tag_ref[0]

    def run(split):
        for head in range(heads):
            base = head * 192

            def chunk(c, carry):
                query = x_ref[pl.ds(c * 8, 8), 0, 0, :, base : base + 64].reshape(256, 64)
                query = query * jnp.asarray(0.125, BF16)
                if split:
                    rows = pl.ds((c // 2) * 16, 16)
                    count = 512
                else:
                    rows = pl.ds(0, 32)
                    count = 1024
                keys = x_ref[rows, 0, 0, :, base + 64 : base + 128].reshape(count, 64)
                values = x_ref[rows, 0, 0, :, base + 128 : base + 192].reshape(count, 64)
                scores = dot_nt(query, keys)
                if split:
                    qj = lax.broadcasted_iota(jnp.int32, (256, count), 0) & 16
                    kj = lax.broadcasted_iota(jnp.int32, (256, count), 1) & 16
                    scores = jnp.where(qj == kj, scores, -1e30)
                top = jnp.max(scores, axis=-1, keepdims=True)
                expo = jnp.exp(scores - top)
                total = jnp.sum(expo, axis=-1, keepdims=True)
                out = dot_nn(expo.astype(BF16), values) / total
                o_ref[pl.ds(c * 8, 8), 0, 0, :, head * 64 : head * 64 + 64] = out.astype(BF16).reshape(8, 32, 64)
                lse_ref[0, head : head + 1, pl.ds(pl.multiple_of(c * 256, 256), 256)] = to_row(top + jnp.log(total), 256)
                return carry

            lax.fori_loop(0, 4, chunk, 0)

    pl.when(tag == 1)(lambda: run(False))
    pl.when(tag != 1)(lambda: run(True))


def group_block(width):
    return pl.BlockSpec((32, 1, 1, 32, width), lambda g: (0, g // 2, g % 2, 0, 0))


def attend_stage(tag, mixed_qkv, heads):
    view = mixed_qkv.reshape(32, 2, 2, 32, 192 * heads)
    out, lse = pl.pallas_call(
        partial(attend_kernel, heads=heads),
        grid=(4,),
        in_specs=[pl.BlockSpec(memory_space=pltpu.SMEM), group_block(192 * heads)],
        out_specs=[group_block(64 * heads), pl.BlockSpec((1, 8, 1024), lambda g: (g, 0, 0))],
        out_shape=[
            jax.ShapeDtypeStruct((32, 2, 2, 32, 64 * heads), BF16),
            jax.ShapeDtypeStruct((4, 8, 1024), F32),
        ],
        compiler_params=pltpu.CompilerParams(vmem_limit_bytes=VMEM_MAX),
        name="attend_stage",
    )(tag, view)
    return out, lse


def attend_back_kernel(tag_ref, x_ref, o_ref, do_ref, lse_ref, g_ref, acc_ref, *, heads):
    tag = tag_ref[0]

    def run(split):
        for head in range(heads):
            base = head * 192
            acc_ref[...] = jnp.zeros_like(acc_ref)

            def chunk(c, carry):
                mine = pl.ds(c * 8, 8)
                query = x_ref[mine, 0, 0, :, base : base + 64].reshape(256, 64)
                query = query * jnp.asarray(0.125, BF16)
                grad = do_ref[mine, 0, 0, :, head * 64 : head * 64 + 64].reshape(256, 64)
                out = o_ref[mine, 0, 0, :, head * 64 : head * 64 + 64].reshape(256, 64)
                if split:
                    first = (c // 2) * 16
                    count = 512
                else:
                    first = 0
                    count = 1024
                rows = pl.ds(first, count // 32)
                keys = x_ref[rows, 0, 0, :, base + 64 : base + 128].reshape(count, 64)
                values = x_ref[rows, 0, 0, :, base + 128 : base + 192].reshape(count, 64)
                lse = lse_ref[0, head : head + 1, pl.ds(pl.multiple_of(c * 256, 256), 256)]
                delta = jnp.sum(grad.astype(F32) * out.astype(F32), axis=-1, keepdims=True)
                delta = to_row(delta, 256)
                probs = jnp.exp(dot_nt(keys, query) - lse)
                if split:
                    qj = lax.broadcasted_iota(jnp.int32, (count, 256), 1) & 16
                    kj = lax.broadcasted_iota(jnp.int32, (count, 256), 0) & 16
                    probs = jnp.where(qj == kj, probs, 0.0)
                scores = (probs * (dot_nt(values, grad) - delta)).astype(BF16)
                zero = jnp.zeros((256, 64), BF16)
                part = dot_nn(scores, jnp.concatenate([query, zero], axis=1))
                part += dot_nn(probs.astype(BF16), jnp.concatenate([zero, grad], axis=1))
                target = pl.ds(pl.multiple_of(first * 32, 256), count)
                acc_ref[target, :] += part
                grad_query = dot_tn(scores, keys) * 0.125
                g_ref[mine, 0, 0, :, base : base + 64] = grad_query.reshape(8, 32, 64)
                return carry

            lax.fori_loop(0, 4, chunk, 0)
            g_ref[:, 0, 0, :, base + 64 : base + 192] = acc_ref[...].reshape(32, 32, 128)

    pl.when(tag == 1)(lambda: run(False))
    pl.when(tag != 1)(lambda: run(True))


def attend_back_stage(tag, mixed_qkv, heads_out, grad_heads, lse, heads):
    view = mixed_qkv.reshape(32, 2, 2, 32, 192 * heads)
    grads = grad_heads.reshape(32, 2, 2, 32, 64 * heads)
    out = pl.pallas_call(
        partial(attend_back_kernel, heads=heads),
        grid=(4,),
        in_specs=[
            pl.BlockSpec(memory_space=pltpu.SMEM),
            group_block(192 * heads),
            group_block(64 * heads),
            group_block(64 * heads),
            pl.BlockSpec((1, 8, 1024), lambda g: (g, 0, 0)),
        ],
        out_specs=group_block(192 * heads),
        out_shape=jax.ShapeDtypeStruct((32, 2, 2, 32, 192 * heads), F32),
        scratch_shapes=[pltpu.VMEM((1024, 128), F32)],
        compiler_params=pltpu.CompilerParams(vmem_limit_bytes=VMEM_MAX),
        name="attend_back_stage",
    )(tag, view, heads_out, grads, lse)
    return out.reshape(TOK, 192 * heads)


def kernel_sums(acc, even, odd, odd_left, even_right, plain, scale, first):
    plain_e, plain_o = plain

    def fold(values):
        return jnp.sum(values.reshape(4, 8, values.shape[-1]), axis=0)

    terms = [
        fold(odd * plain_e) + fold(even_right * plain_o),
        fold(even * plain_e) + fold(odd * plain_o),
        fold(odd_left * plain_e) + fold(even * plain_o),
    ]
    out = list(acc)
    for t in range(3):
        term = terms[t] if scale is None else terms[t] * scale
        out[first + t] = acc[first + t] + term
    return out


POLY = (
    0.13241715506535054,
    0.12108811680396304,
    0.17555028579228482,
    -0.0796444980816301,
    0.3217932733518851,
    -0.21571441684424994,
    0.04451008654080756,
)


def gelu_parts(z):
    size = jnp.abs(z)
    t = 1.0 / (1.0 + 0.33 * size)
    expo = jnp.exp(z * z * -0.5)
    poly = POLY[6]
    for c in POLY[5::-1]:
        poly = poly * t + c
    tail = poly * t * expo
    cdf = jnp.where(z >= 0.0, 1.0 - tail, tail)
    value = z * cdf
    slope = cdf + z * (expo * 0.3989422804014327)
    return value, slope


def feed_kernel(
    info_ref,
    heads_ref,
    w_out_ref,
    tok_ref,
    cot_ref,
    mods_ref,
    w_up_ref,
    w_down_ref,
    taps_ref,
    perm_ref,
    mixed_ref,
    gheads_ref,
    gup_ref,
    gdown_ref,
    gout_ref,
    gtaps_ref,
    gafter_ref,
    sums_ref,
    after_ref,
    att_ref,
    hidden_ref,
    hidden_t,
    gfeed_ref,
    gfeed_t,
    feed_ref,
    ghid_ref,
    up_ref,
    slope_ref,
    act_ref,
    gupw_ref,
    sum_ref,
):
    step = pl.program_id(0)
    tag = info_ref[0]
    first_row = info_ref[1] * QROWS - HALO
    chans = up_ref.shape[1]
    groups = heads_ref.shape[0]

    def mod(i):
        return mods_ref[:, i * D : (i + 1) * D]

    @pl.when(step == 0)
    def _():
        gate_one, shift_two, scale_two, gate_two = mod(2), mod(3), 1.0 + mod(4), mod(5)

        def part(start, size):
            rows = pl.ds(start, size)
            perm = perm_ref[0:size, 0:size]
            ordered = dot_nn(perm, tok_ref[rows, :])
            attention = jnp.zeros((size, D), F32)
            for g in range(groups):
                term = dot_nn(heads_ref[g, rows, :], w_out_ref[g])
                attention = attention + term.astype(BF16).astype(F32)
            att_ref[rows, :] = attention
            after = ordered + by_half(attention, gate_one)
            after_ref[rows, :] = after
            unit, _ = normalised(after)
            hidden_ref[rows, :] = (by_half(unit, scale_two) + spread(shift_two, size)).astype(BF16)
            gfeed_ref[rows, :] = by_half(dot_nn(perm, cot_ref[rows, :]), gate_two).astype(BF16)

        part(0, 128)
        part(XTOK - 128, 128)

        def loop(i, carry):
            part(pl.multiple_of(128 + i * 256, 128), 256)
            return carry

        lax.fori_loop(0, 4, loop, 0)
        hidden_t[...] = jnp.transpose(hidden_ref[pl.ds(128, QTOK), :])
        gfeed_t[...] = jnp.transpose(gfeed_ref[pl.ds(128, QTOK), :])
        feed_ref[...] = jnp.zeros_like(feed_ref)
        ghid_ref[...] = jnp.zeros_like(ghid_ref)

    w_up = w_up_ref[...].reshape(D, chans)
    w_down = w_down_ref[...].reshape(chans, D)

    def up_loop(i, carry):
        rows = pl.ds(pl.multiple_of(i * 640, 128), 640)
        up_ref[rows, :] = dot_nn(hidden_ref[rows, :], w_up)
        return carry

    lax.fori_loop(0, 2, up_loop, 0)

    for lane in range(0, chans, 128):
        lanes = slice(lane, lane + 128)
        masks = column_masks(tag, 128)
        taps = [taps_ref[0, t : t + 1, lanes] for t in range(9)]

        def one(n, carry):
            start = pl.multiple_of(n * SIDE, SIDE)
            even = up_ref[pl.ds(start, 32), lanes]
            odd = up_ref[pl.ds(start + 32, 32), lanes]
            down, up = row_scales(tag, first_row + n)
            done, carry, _ = conv_step(even, odd, masks, taps, down, up, carry)
            return done, carry

        def loop(n, carry):
            done, carry = one(n, carry)
            for k in range(2):
                start = pl.multiple_of((n - 2) * SIDE + 32 * k, 32)
                value, slope = gelu_parts(done[k])
                act_ref[pl.ds(start, 32), lanes] = value.astype(BF16)
                slope_ref[pl.ds(start, 32), lanes] = slope
            return carry

        _, carry = one(0, no_carry(128))
        _, carry = one(1, carry)
        lax.fori_loop(2, QROWS + 2 * HALO, loop, carry)

    def gact_loop(i, carry):
        rows = pl.ds(pl.multiple_of(i * 576, 64), 576)
        out = dot_nt(gfeed_ref[pl.ds(pl.multiple_of(64 + i * 576, 64), 576), :], w_down)
        slope_ref[rows, :] = out * slope_ref[rows, :]
        return carry

    lax.fori_loop(0, 2, gact_loop, 0)

    for lane in range(0, chans, 128):
        lanes = slice(lane, lane + 128)
        masks = column_masks(tag, 128)
        taps = [taps_ref[0, 8 - t : 9 - t, lanes] for t in range(9)]

        def one(n, carry, sums):
            start = pl.multiple_of(n * SIDE, SIDE)
            low, high = pl.ds(start, 32), pl.ds(start + 32, 32)
            even, odd = slope_ref[low, lanes], slope_ref[high, lanes]
            row = first_row + 1 + n
            down, up = row_scales(tag, row)
            done, carry, shifted = conv_step(even, odd, masks, taps, down, up, carry)
            if sums is not None:
                above = jnp.where((row == 0) | ((tag == 0) & (row == 32)), 0.0, 1.0)
                below = jnp.where((row == SIDE - 1) | ((tag == 0) & (row == 31)), 0.0, 1.0)
                for i, scale in ((0, above), (1, None), (2, below)):
                    at = pl.multiple_of((n + i) * SIDE, SIDE)
                    plain = (up_ref[pl.ds(at, 32), lanes], up_ref[pl.ds(at + 32, 32), lanes])
                    sums = kernel_sums(sums, even, odd, *shifted, plain, scale, 3 * i)
            return done, carry, sums

        def put(n, done):
            for k in range(2):
                start = pl.multiple_of((n - 2) * SIDE + 32 * k, 32)
                gupw_ref[pl.ds(start, 32), lanes] = done[k].astype(BF16)

        def loop(n, state):
            done, carry, sums = one(n, state[0], list(state[1]))
            put(n, done)
            return carry, tuple(sums)

        zero = jnp.zeros((8, 128), F32)
        _, carry, _ = one(0, no_carry(128), None)
        _, carry, sums = one(1, carry, [zero] * 9)
        carry, sums = lax.fori_loop(2, QROWS + 1, loop, (carry, tuple(sums)))
        done, carry, _ = one(QROWS + 1, carry, None)
        put(QROWS + 1, done)
        for t in range(9):
            gtaps_ref[0, t : t + 1, lanes] = jnp.sum(sums[t], axis=0, keepdims=True)

    def token_loop(i, carry):
        rows = pl.ds(pl.multiple_of(i * 512, 512), 512)
        feed_ref[rows, :] += dot_nn(act_ref[pl.ds(pl.multiple_of(64 + i * 512, 64), 512), :], w_down)
        ghid_ref[rows, :] += dot_nt(gupw_ref[rows, :], w_up)
        return carry

    lax.fori_loop(0, 2, token_loop, 0)
    dps, per = gup_ref.shape[0], gup_ref.shape[2]

    def weight_loop(i, carry):
        rows = pl.ds(pl.multiple_of(i * 384, 128), 384)
        blocks = pl.ds(i * (dps // 2), dps // 2)
        out = dot_nn(hidden_t[rows, :], gupw_ref[...])
        gup_ref[blocks, 0, :, :] = out.reshape(dps // 2, per, chans).astype(gup_ref.dtype)
        out = dot_nn(gfeed_t[rows, :], act_ref[pl.ds(64, QTOK), :])
        gdown_ref[blocks, 0, :, :] = out.reshape(dps // 2, per, chans).astype(gdown_ref.dtype)
        return carry

    lax.fori_loop(0, 2, weight_loop, 0)

    @pl.when(step == pl.num_programs(0) - 1)
    def _():
        gate_one, scale_two, gate_two = mod(2), 1.0 + mod(4), mod(5)
        sum_ref[...] = jnp.zeros_like(sum_ref)

        def loop(i, carry):
            rows = pl.ds(pl.multiple_of(i * 256, 256), 256)
            wide = pl.ds(pl.multiple_of(128 + i * 256, 128), 256)
            after = after_ref[wide, :]
            feed = feed_ref[rows, :]
            result = (after + by_half(feed, gate_two)).astype(BF16)
            mixed_ref[rows, :] = dot_tn(perm_ref[...], result).astype(BF16)
            cot = dot_nn(perm_ref[...], cot_ref[wide, :])
            sum_ref[3] += half_sums(cot * feed)
            unit, rstd = normalised(after)
            grad = ghid_ref[rows, :]
            sum_ref[1] += half_sums(grad)
            sum_ref[2] += half_sums(grad * unit)
            inner = by_half(grad, scale_two)
            mean = jnp.mean(inner, axis=-1, keepdims=True)
            along = jnp.mean(inner * unit, axis=-1, keepdims=True)
            gafter = cot + rstd * (inner - mean - unit * along)
            sum_ref[0] += half_sums(gafter * att_ref[wide, :])
            gafter_ref[rows, :] = gafter
            gatt = by_half(gafter, gate_one).astype(BF16)
            gupw_ref[rows, :] = gatt
            for g in range(groups):
                gheads_ref[g, rows, :] = dot_nt(gatt, w_out_ref[g]).astype(BF16)
            return carry

        lax.fori_loop(0, 4, loop, 0)
        for g in range(groups):
            out = dot_tn(gupw_ref[...], heads_ref[g, pl.ds(128, QTOK), :])
            gout_ref[:, g, :, :] = out.reshape(dps, per, out.shape[-1]).astype(gout_ref.dtype)
        sums_ref[...] = jnp.sum(sum_ref[...], axis=2)


def feed_stage(info, heads, w_out, tok, cot, mods, w_up, w_down, taps, perm, wire):
    groups, _, hwidth = heads.shape
    dps, chunks, per, chans = w_up.shape
    once = pl.Buffered(1)
    whole = lambda shape: pl.BlockSpec(shape, lambda s: (0,) * len(shape), pipeline_mode=once)
    weights = pl.BlockSpec((dps, 1, per, chans), lambda s: (0, s, 0, 0))
    return pl.pallas_call(
        feed_kernel,
        grid=(chunks,),
        in_specs=[
            pl.BlockSpec(memory_space=pltpu.SMEM),
            whole(heads.shape),
            whole(w_out.shape),
            whole((XTOK, D)),
            whole((XTOK, D)),
            whole((2, 6 * D)),
            weights,
            weights,
            pl.BlockSpec((1, 9, chans), lambda s: (s, 0, 0)),
            whole((256, 256)),
        ],
        out_specs=[
            whole((QTOK, D)),
            whole((groups, QTOK, hwidth)),
            weights,
            weights,
            whole((dps, groups, per, hwidth)),
            pl.BlockSpec((1, 9, chans), lambda s: (s, 0, 0)),
            whole((QTOK, D)),
            whole((4, 2, D)),
        ],
        out_shape=[
            jax.ShapeDtypeStruct((QTOK, D), BF16),
            jax.ShapeDtypeStruct((groups, QTOK, hwidth), BF16),
            jax.ShapeDtypeStruct((dps, chunks, per, chans), wire),
            jax.ShapeDtypeStruct((dps, chunks, per, chans), wire),
            jax.ShapeDtypeStruct((dps, groups, per, hwidth), wire),
            jax.ShapeDtypeStruct((chunks, 9, chans), F32),
            jax.ShapeDtypeStruct((QTOK, D), F32),
            jax.ShapeDtypeStruct((4, 2, D), F32),
        ],
        scratch_shapes=[
            pltpu.VMEM((XTOK, D), F32),
            pltpu.VMEM((XTOK, D), F32),
            pltpu.VMEM((XTOK, D), BF16),
            pltpu.VMEM((D, QTOK), BF16),
            pltpu.VMEM((XTOK, D), BF16),
            pltpu.VMEM((D, QTOK), BF16),
            pltpu.VMEM((QTOK, D), F32),
            pltpu.VMEM((QTOK, D), F32),
            pltpu.VMEM((XTOK, chans), F32),
            pltpu.VMEM((XTOK - 128, chans), F32),
            pltpu.VMEM((XTOK - 128, chans), BF16),
            pltpu.VMEM((QTOK, chans), BF16),
            pltpu.VMEM((4, 2, 16, D), F32),
        ],
        compiler_params=pltpu.CompilerParams(vmem_limit_bytes=VMEM_MAX),
        name="feed_stage",
    )(info, heads, w_out, tok, cot, mods, w_up, w_down, taps, perm)


def conv_back_kernel(tag_ref, grad_ref, proj_ref, taps_ref, out_ref, gtaps_ref):
    tag = tag_ref[0]
    width = grad_ref.shape[1]
    for lane in range(0, width, 128):
        size = min(128, width - lane)
        lanes = slice(lane, lane + size)
        masks = column_masks(tag, size)
        taps = [taps_ref[8 - t : 9 - t, lanes] for t in range(9)]

        def one(row, carry, sums, has_above, has_below):
            start = pl.multiple_of(row * SIDE, SIDE)
            even = grad_ref[pl.ds(start, 32), lanes]
            odd = grad_ref[pl.ds(start + 32, 32), lanes]
            down, up = row_scales(tag, row)
            done, carry, shifted = conv_step(even, odd, masks, taps, down, up, carry)
            for i in range(3):
                if (i == 0 and not has_above) or (i == 2 and not has_below):
                    continue
                at = pl.multiple_of((row + i - 1) * SIDE, SIDE)
                plain = (proj_ref[pl.ds(at, 32), lanes], proj_ref[pl.ds(at + 32, 32), lanes])
                scale = (up, None, down)[i]
                sums = kernel_sums(sums, even, odd, *shifted, plain, scale, 3 * i)
            return done, carry, sums

        def put(row, done):
            for k in range(2):
                start = pl.multiple_of(row * SIDE + 32 * k, 32)
                out_ref[pl.ds(start, 32), lanes] = done[k].astype(BF16)

        def loop(row, state):
            done, carry, sums = one(row, state[0], list(state[1]), True, True)
            put(row - 1, done)
            return carry, tuple(sums)

        zero = jnp.zeros((8, size), F32)
        _, carry, sums = one(0, no_carry(size), [zero] * 9, False, True)
        carry, sums = lax.fori_loop(1, SIDE - 1, loop, (carry, tuple(sums)))
        done, carry, sums = one(SIDE - 1, carry, list(sums), True, False)
        put(SIDE - 2, done)
        put(SIDE - 1, carry[0:2])
        for t in range(9):
            gtaps_ref[t : t + 1, lanes] = jnp.sum(sums[t], axis=0, keepdims=True)


def conv_back_stage(tag, grad, proj, taps):
    width = grad.shape[1]
    space = pl.BlockSpec(memory_space=pltpu.VMEM)
    return pl.pallas_call(
        conv_back_kernel,
        in_specs=[pl.BlockSpec(memory_space=pltpu.SMEM), space, space, space],
        out_specs=[space, space],
        out_shape=[jax.ShapeDtypeStruct((TOK, width), BF16), jax.ShapeDtypeStruct((9, width), F32)],
        compiler_params=pltpu.CompilerParams(vmem_limit_bytes=VMEM_MAX),
        name="conv_back_stage",
    )(tag, grad, proj, taps)


def last_kernel(ghid_ref, tok_ref, gafter_ref, mods_ref, perm_ref, out_ref, sums_ref, sum_ref, turn_ref):
    scale = 1.0 + mods_ref[:, D : 2 * D]
    sum_ref[...] = jnp.zeros_like(sum_ref)

    def loop(i, carry):
        rows = pl.ds(pl.multiple_of(i * 256, 256), 256)
        ordered = dot_nn(perm_ref[...], tok_ref[rows, :])
        unit, rstd = normalised(ordered)
        grad = ghid_ref[rows, :].astype(F32)
        sum_ref[0] += half_sums(grad)
        sum_ref[1] += half_sums(grad * unit)
        inner = by_half(grad, scale)
        mean = jnp.mean(inner, axis=-1, keepdims=True)
        along = jnp.mean(inner * unit, axis=-1, keepdims=True)
        out = gafter_ref[rows, :] + rstd * (inner - mean - unit * along)
        for lane in range(D // 128):
            for r in range(4):
                for parity in range(2):
                    at = r * 64 + parity * 32
                    turn_ref[lane, pl.ds(r * 64 + parity, 32, stride=2), :] = out[
                        at : at + 32, lane * 128 : lane * 128 + 128
                    ]
            out_ref[rows, lane * 128 : lane * 128 + 128] = turn_ref[lane]
        return carry

    lax.fori_loop(0, QTOK // 256, loop, 0)
    sums_ref[...] = jnp.sum(sum_ref[...], axis=2)


def last_stage(ghid, tok, gafter, mods, perm):
    space = pl.BlockSpec(memory_space=pltpu.VMEM)
    return pl.pallas_call(
        last_kernel,
        in_specs=[space] * 5,
        out_specs=[space] * 2,
        out_shape=[jax.ShapeDtypeStruct((QTOK, D), F32), jax.ShapeDtypeStruct((2, 2, D), F32)],
        scratch_shapes=[pltpu.VMEM((2, 2, 16, D), F32), pltpu.VMEM((D // 128, 256, 128), F32)],
        compiler_params=pltpu.CompilerParams(vmem_limit_bytes=VMEM_MAX),
        name="last_stage",
    )(ghid, tok, gafter, mods, perm)


def per_device(
    tokens,
    cotangent,
    size_tags,
    time_index,
    class_index,
    time_table,
    class_table,
    w_mod,
    w_qkv,
    conv_qkv,
    w_out,
    w_up,
    conv_ffn,
    w_down,
):
    tp_count = lax.axis_size("tp")
    dp_count = lax.axis_size("dp")
    tp_rank = lax.axis_index("tp")
    dp_rank = lax.axis_index("dp")
    tag = size_tags[0]
    heads = w_out.shape[0] // HEAD_SIZE
    perm = parity_matrix()
    share = D // dp_count
    fold = 8

    def gather_weights(weight):
        mine = lax.dynamic_slice_in_dim(weight, dp_rank * share, share, 0)
        stacked = lax.all_gather(mine, "tp", axis=0)
        stacked = lax.all_gather(stacked, "dp", axis=0)
        if dp_count == fold:
            return stacked
        inner = stacked.reshape(fold, dp_count // fold, tp_count, share, D)
        return inner.transpose(0, 2, 1, 3, 4).reshape(fold, tp_count, D // fold, D)

    w_up_all = gather_weights(w_up)
    w_down_all = gather_weights(w_down)
    w_out_all = lax.all_gather(w_out, "tp", axis=0)
    conv_ffn_all = lax.all_gather(conv_ffn, "tp", axis=0).astype(F32)

    time_rows = jnp.take(time_table, time_index, axis=0).astype(F32)
    class_rows = jnp.take(class_table, class_index, axis=0).astype(F32)
    condition_all = time_rows + class_rows
    activated_all = jax.nn.silu(condition_all).astype(BF16)
    activated = lax.dynamic_slice_in_dim(activated_all, dp_rank * SLOTS, SLOTS, 0)
    mod_part = jnp.dot(activated, w_mod, preferred_element_type=F32)
    modulation = lax.all_gather(mod_part, "tp", axis=1, tiled=True)
    per_quad = jnp.where(tag == 1, jnp.broadcast_to(modulation[0:1], modulation.shape), modulation)
    quads = per_quad.reshape(2, 2, 6 * D)
    quad_row = tp_rank * QROWS // (SIDE // 2)
    mods = lax.dynamic_index_in_dim(quads, quad_row, 0, keepdims=False)

    tag_word = size_tags.astype(jnp.int32)
    taps_qkv = conv_qkv.astype(F32)
    hidden_one, projected, mixed_qkv = first_stage(
        tag_word, tokens, quads[..., 0:D], quads[..., D : 2 * D], w_qkv, taps_qkv, perm
    )
    heads_out, lse = attend_stage(tag_word, mixed_qkv, heads)

    pad = ((HALO * SIDE, HALO * SIDE), (0, 0))
    flat_heads = jnp.pad(heads_out.reshape(TOK, heads * HEAD_SIZE), pad)
    sends = jnp.stack([flat_heads[k * QTOK : k * QTOK + XTOK] for k in range(tp_count)])
    heads_in = lax.all_to_all(sends, "tp", split_axis=0, concat_axis=0, tiled=True)
    tok_wide = lax.dynamic_slice_in_dim(jnp.pad(tokens, pad), tp_rank * QTOK, XTOK, 0)
    cot_wide = lax.dynamic_slice_in_dim(jnp.pad(cotangent, pad), tp_rank * QTOK, XTOK, 0)
    info = jnp.stack([tag, tp_rank]).astype(jnp.int32)
    wire = BF16
    mixed_q, gheads, g_up, g_down, g_out, g_taps_ffn, g_after, sums_two = feed_stage(
        info, heads_in, w_out_all, tok_wide, cot_wide, mods, w_up_all, w_down_all, conv_ffn_all, perm, wire
    )
    grad_heads = lax.all_to_all(gheads, "tp", split_axis=0, concat_axis=0, tiled=True)
    grad_heads = grad_heads.reshape(TOK, heads * HEAD_SIZE)
    mixed = lax.all_gather(mixed_q, "tp", axis=0, tiled=True)

    grad_mixed = attend_back_stage(tag_word, mixed_qkv, heads_out, grad_heads, lse, heads)
    grad_proj, g_taps_qkv = conv_back_stage(tag_word, grad_mixed, projected, taps_qkv)
    ghid_part = jnp.dot(grad_proj, w_qkv.T, preferred_element_type=F32).astype(BF16)
    ghid_one = lax.psum_scatter(ghid_part, "tp", scatter_dimension=0, tiled=True)
    grad_qkv_w = jnp.einsum("td,tc->dc", hidden_one, grad_proj, preferred_element_type=F32)
    summed_qkv = lax.psum_scatter(grad_qkv_w, "dp", scatter_dimension=0, tiled=True)

    tok_mine = lax.dynamic_slice_in_dim(tokens, tp_rank * QTOK, QTOK, 0)
    grad_tokens, sums_one = last_stage(ghid_one, tok_mine, g_after, mods, perm)

    def reduce_rows(grads):
        if dp_count != fold:
            inner = grads.reshape(fold, tp_count, dp_count // fold, share, grads.shape[-1])
            grads = inner.transpose(0, 2, 1, 3, 4).reshape(dp_count, tp_count, share, grads.shape[-1])
        mine = lax.psum_scatter(grads, "dp", scatter_dimension=0, tiled=True)[0]
        return lax.psum_scatter(mine, "tp", scatter_dimension=0, tiled=True)[0].astype(F32)

    summed_up = reduce_rows(g_up)
    summed_down = reduce_rows(g_down).T
    summed_out = reduce_rows(g_out).T
    mine_taps = lax.psum_scatter(g_taps_ffn, "tp", scatter_dimension=0, tiled=True)[0]
    summed_conv_ffn = lax.psum_scatter(mine_taps, "dp", scatter_dimension=1, tiled=True)
    summed_conv_qkv = lax.psum_scatter(g_taps_qkv, "dp", scatter_dimension=1, tiled=True)

    quad_rows = jnp.concatenate(
        [sums_one[0], sums_one[1], sums_two[0], sums_two[1], sums_two[2], sums_two[3]], axis=-1
    )
    row_pick = (lax.iota(jnp.int32, 2) == quad_row)[:, None, None]
    grad_quads = jnp.where(row_pick, quad_rows[None], 0.0).reshape(4, 6 * D)
    merged = jnp.concatenate(
        [jnp.sum(grad_quads, axis=0, keepdims=True), jnp.zeros((SLOTS - 1, 6 * D), F32)], axis=0
    )
    grad_slots = jnp.where(tag == 1, merged, grad_quads)
    slot_cols = lax.psum_scatter(grad_slots, "tp", scatter_dimension=1, tiled=True)
    mod_cols = lax.all_gather(slot_cols, "dp", axis=0, tiled=True)
    my_act = lax.dynamic_slice_in_dim(activated_all, dp_rank * share, share, 1).astype(F32)
    my_cond = lax.dynamic_slice_in_dim(condition_all, dp_rank * share, share, 1)
    my_w_mod = lax.dynamic_slice_in_dim(w_mod, dp_rank * share, share, 0).astype(F32)
    summed_mod = jnp.dot(my_act.T, mod_cols, precision=lax.Precision.HIGHEST)
    part_act = jnp.dot(mod_cols, my_w_mod.T, precision=lax.Precision.HIGHEST)
    grad_act = lax.psum(part_act, "tp")
    _, silu_pull = jax.vjp(jax.nn.silu, my_cond)
    grad_cols = silu_pull(grad_act)[0]
    time_iota = lax.broadcasted_iota(jnp.int32, (time_index.shape[0], time_table.shape[0]), 1)
    time_hits = (time_index[:, None] == time_iota).astype(F32)
    grad_time = jnp.dot(time_hits.T, grad_cols, precision=lax.Precision.HIGHEST)
    class_iota = lax.broadcasted_iota(jnp.int32, (class_index.shape[0], class_table.shape[0]), 1)
    class_hits = (class_index[:, None] == class_iota).astype(F32)
    grad_class = jnp.dot(class_hits.T, grad_cols, precision=lax.Precision.HIGHEST)
    return (
        mixed,
        grad_tokens,
        grad_time,
        grad_class,
        summed_mod,
        summed_qkv,
        summed_conv_qkv,
        summed_out,
        summed_up,
        summed_conv_ffn,
        summed_down,
    )


def solution(mesh):
    in_specs = (
        P("dp", None),
        P("dp", None),
        P("dp"),
        P(),
        P(),
        P(),
        P(),
        P(None, "tp"),
        P(None, "tp"),
        P(None, "tp"),
        P("tp", None),
        P(None, "tp"),
        P(None, "tp"),
        P("tp", None),
    )
    out_specs = (
        P("dp", None),
        P(("dp", "tp"), None),
        P(None, "dp"),
        P(None, "dp"),
        P("dp", "tp"),
        P("dp", "tp"),
        P(None, ("tp", "dp")),
        P("tp", "dp"),
        P("dp", "tp"),
        P(None, ("tp", "dp")),
        P("tp", "dp"),
    )
    return jax.shard_map(
        per_device, mesh=mesh, in_specs=in_specs, out_specs=out_specs, check_vma=False
    )
```

time: 1980 us -> 940 us (0.47)
  waiting for transfers between devices: 929 us -> 393 us
  other arithmetic: 493 us -> 8.51 us
  matrix products: 281 us -> 26.4 us
  Pallas kernels: 0 us -> 242 us
  blocking collectives: 57.2 us -> 196 us
  local copies, waits for them, and re-layouts: 184 us -> 46.4 us
    psum x2 -> x0, waiting for transfers between devices: 446 us -> none  [the longest x1 224 us: per_device(): lax.psum(jnp.dot(heads_out, w_out, preferred_element_type=jnp.float32).as...]
    dot_general x42 -> x5, matrix products: 272 us -> 22.5 us  [the longest x1 9.84 us: per_device(): jnp.einsum('td,tc->dc', hidden_one, grad_proj, preferred_element_type=F32)]
    pallas_call x0 -> x6, Pallas kernels: none -> 242 us  [the longest x1 108 us: feed_stage(): pl.pallas_call(feed_kernel, grid=(chunks,), in_specs=[pl.BlockSpec(memory...]
    convert_element_type x18 -> x4, other arithmetic: 193 us -> 3.69 us  [the longest x1 1.64 us: reduce_rows(): lax.psum_scatter(mine, 'tp', scatter_dimension=0, tiled=True)[0].astype(F32)]
    reduce_sum x19 -> x0, other arithmetic: 126 us -> none  [the longest x1 43.9 us: depthwise(): kernel[tap_index]]
    all_gather x0 -> x4, blocking collectives: none -> 101 us  [the longest x2 46.1 us: gather_weights(): stacked = lax.all_gather(mine, 'tp', axis=0)]
    reduce_scatter x5 -> x8, waiting for transfers between devices: 298 us -> 204 us  [the longest x1 109 us: per_device(): lax.psum_scatter(ghid_part, 'tp', scatter_dimension=0, tiled=True)]
    another operation x4 -> x3, local copies, waits for them, and re-layouts: 66.8 us -> 0.53 us  [per_device(): jnp.stack([flat_heads[k * QTOK:k * QTOK + XTOK] for k in range(tp_count)])]
  transfers between devices with their start and end apart: 13 -> 16, of which waited for: 11 -> 8; matrix products, arithmetic and copies ran while one was open for 5% -> 8% of each run, Pallas kernels for 0% -> 14%
where the time goes in v1:
time: 940 us; the launch traced here: 933 us
  waiting for transfers between devices  393 us (42%)
  Pallas kernels  242 us (26%)
  blocking collectives  196 us (21%)
  local copies, waits for them, and re-layouts  46.4 us (5%)
  matrix products  26.4 us (3%)
  between operations  16.1 us (2%)
    all_gather x1, waiting for transfers between devices, per_device(): mixed = lax.all_gather(mixed_q, 'tp', axis=0, tiled=True)  114 us
    reduce_scatter x1, waiting for transfers between devices, per_device(): lax.psum_scatter(ghid_part, 'tp', scatter_dimension=0, tiled=True)  109 us
    pallas_call x1, Pallas kernels, feed_stage(): pl.pallas_call(feed_kernel, grid=(chunks,), in_specs=[pl.BlockSpec(memory...  108 us
    unnamed x17, waiting for transfers between devices  66.7 us
    reduce_scatter x3, waiting for transfers between devices, reduce_rows(): mine = lax.psum_scatter(grads, 'dp', scatter_dimension=0, tiled=True)[0]  55.8 us
    all_gather x2, blocking collectives, gather_weights(): stacked = lax.all_gather(mine, 'tp', axis=0)  46.1 us
    all_gather x1, blocking collectives, per_device(): conv_ffn_all = lax.all_gather(conv_ffn, 'tp', axis=0).astype(F32)  45.8 us
    all_to_all x1, blocking collectives, per_device(): lax.all_to_all(gheads, 'tp', split_axis=0, concat_axis=0, tiled=True)  40.8 us
  transfers between devices with their start and end apart: 16, of which 8 were waited for; matrix products, arithmetic and copies ran while one was open for 8% of the time, Pallas kernels for 14%

profile of v1, /device:TPU:0, one launch (start us, length us, event | category | flops | bytes accessed | tf_op | source)
XLA Modules:
  0.0 933.2 jit_solution(7605910393381115909)
XLA Ops:
  8.9 22.8 %all-gather.1 = bf16[384,768]{1,0:T(8,128)(2,1)} all-gather(bf16[96,768]{1,0:T(8,128)(2,1)S(1)} %constant_dynamic-slice_fusion.2), channel_id=3, replica_groups=mesh['dp'=8,'tp'=4] {'tp'}, dimensions={0}, use_global_device_ids=true | all-gather | bytes 737280 | tf_op jit(solution)/shard_map/all_gather | solution.py:780
  32.7 23.3 %all-gather.3 = bf16[384,768]{1,0:T(8,128)(2,1)} all-gather(bf16[96,768]{1,0:T(8,128)(2,1)S(1)} %constant_dynamic-slice_fusion.1), channel_id=5, replica_groups=mesh['dp'=8,'tp'=4] {'tp'}, dimensions={0}, use_global_device_ids=true | all-gather | bytes 737280 | tf_op jit(solution)/shard_map/all_gather | solution.py:780
  62.4 13.2 %all_gather.45 = f32[4,4608]{1,0:T(4,128)S(1)} all-gather(f32[4,1152]{1,0:T(4,128)S(1)} %fusion.12), channel_id=1, replica_groups=mesh['dp'=8,'tp'=4] {'tp'}, dimensions={1}, use_global_device_ids=true | all-gather | bytes 92160 | tf_op jit(solution)/shard_map/all_gather | solution.py:798
  78.3 30.7 %first_stage.1 = (bf16[4096,768]{1,0:T(8,128)(2,1)}, f32[4096,576]{1,0:T(8,128)}, bf16[4096,576]{1,0:T(8,128)(2,1)}) custom-call(s32[1]{0:T(128)S(6)} %copy.48.tag_ref, bf16[4096,768]{1,0:T(8,128)(2,1)} %tok_ref.1, f32[2,2,768]{2,1,0:T(2,128)} %get-tuple-element.75.shift_ref, f32[2,2,768]{2,1,0:T(2,128)} %get-tuple-element.74.scale_ref, ...), custom_call_target="tpu_custom_call" | custom-call | tf_op jit(solution)/shard_map/first_stage/pallas_call | solution.py:174
  109.0 29.6 %attend_stage.1 = (bf16[32,2,2,32,192]{4,3,2,1,0:T(8,128)(2,1)}, f32[4,8,1024]{2,1,0:T(8,128)}) custom-call(s32[1]{0:T(128)S(6)} %copy.48.tag_ref, bf16[32,2,2,32,576]{4,3,2,1,0:T(8,128)(2,1)} %bitcast.65), custom_call_target="tpu_custom_call" | custom-call | tf_op jit(solution)/shard_map/attend_stage/pallas_call | solution.py:249
  138.6 4.0 copy.29
  145.9 3.7 all-to-all-start
  149.7 45.8 %all-gather.6 = bf16[4,9,768]{2,1,0:T(8,128)(2,1)S(1)} all-gather(bf16[1,9,768]{2,1,0:T(8,128)(2,1)S(1)} %bitcast.85), channel_id=7, replica_groups=mesh['dp'=8,'tp'=4] {'tp'}, dimensions={0}, use_global_device_ids=true | all-gather | bytes 69120 | tf_op jit(solution)/shard_map/all_gather | solution.py:790
  196.8 4.2 pad_dynamic-slice_fusion
  201.6 2.5 copy.32.heads_ref
  204.1 108.4 %feed_stage.1 = (bf16[1024,768]{1,0:T(8,128)(2,1)}, bf16[4,1024,192]{2,1,0:T(8,128)(2,1)}, bf16[8,4,96,768]{3,2,1,0:T(8,128)(2,1)}, bf16[8,4,96,768]{3,2,1,0:T(8...) custom-call(s32[2]{0:T(128)} %pad_add_fusion.info_ref, ...), custom_call_target="tpu_custom_call" | custom-call | tf_op jit(solution)/shard_map/feed_stage/pallas_call | solution.py:598
  314.8 2.9 copy.33
  317.7 40.8 %all_to_all.10 = bf16[4,1024,192]{1,2,0:T(8,128)(2,1)S(1)} all-to-all(bf16[4,1024,192]{1,2,0:T(8,128)(2,1)S(1)} %copy.33), channel_id=1, replica_groups=mesh['dp'=8,'tp'=4] {'tp'}, dimensions={0} | all-to-all | bytes 3145728 | tf_op jit(solution)/shard_map/all_to_all | solution.py:822
  358.5 2.5 copy.34
  361.0 39.0 %attend_back_stage.1 = f32[32,2,2,32,576]{4,3,2,1,0:T(8,128)} custom-call(s32[1]{0:T(128)S(6)} %copy.48.tag_ref, bf16[32,2,2,32,576]{4,3,2,1,0:T(8,128)(2,1)} %bitcast.66, bf16[32,2,2,32,192]{4,3,2,1,0:T(8,128)(2,1)} %get-tuple-element.30.o_ref, bf16[32,2,2,32,192]{4,3,2,1,0:T(8,128)(2,1)} %bitcast.69, f32[4,8,1024]{2,1,0:T(8,128)} %get-tuple-element.33.lse_ref), custom_call_target="tpu_custom_call" | custom-call | tf_op jit(solution)/shard_map/attend_back_stage/pallas_call | solution.py:315
  400.0 26.5 %conv_back_stage.1 = (bf16[4096,576]{1,0:T(8,128)(2,1)}, f32[9,576]{1,0:T(8,128)}) custom-call(s32[1]{0:T(128)S(6)} %copy.48.tag_ref, f32[4096,576]{1,0:T(8,128)} %bitcast.64, f32[4096,576]{1,0:T(8,128)} %get-tuple-element.34.proj_ref, f32[9,576]{1,0:T(8,128)} %convert_element_type.44.taps_ref), custom_call_target="tpu_custom_call" | custom-call | tf_op jit(solution)/shard_map/conv_back_stage/pallas_call | solution.py:700
  426.5 9.8 %convolution_convert_fusion = bf16[4096,768]{1,0:T(8,128)(2,1)} fusion(bf16[4096,576]{1,0:T(8,128)(2,1)} %get-tuple-element.35, bf16[768,576]{0,1:T(8,128)(2,1)S(1)} %copy-done.4), kind=kOutput, calls=%fused_computation.2 | convolution fusion | flops 3627024384 | bytes 11894784 | tf_op jit(solution)/shard_map/dot_general | solution.py:828
  439.5 55.8 %reduce-scatter.31.cloned.1.call-done = bf16[1,4,96,768]{3,2,1,0:T(8,128)(2,1)} async-done(((bf16[8,4,96,768]{3,2,1,0:T(8,128)(2,1)}), bf16[1,4,96,768]{3,2,1,0:T(8,128)(2,1)}) %reduce-scatter.31.cloned.1.call-update) | async-done | bytes 589840 | tf_op jit(solution)/shard_map/reduce_scatter | solution.py:840
  496.3 2.7 constant_dynamic-slice_fusion.tok_ref
  499.0 109.4 %reduce-scatter.17.cloned.1.call-done.ghid_ref = bf16[1024,768]{1,0:T(8,128)(2,1)} async-done(((bf16[4096,768]{1,0:T(8,128)(2,1)}), bf16[1024,768]{1,0:T(8,128)(2,1)}) %reduce-scatter.17.cloned.1.call-update) | async-done | bytes 1572880 | tf_op jit(solution)/shard_map/reduce_scatter | solution.py:829
  608.4 7.9 last_stage.1
  620.6 9.8 %fusion.21 = f32[768,576]{1,0:T(8,128)} fusion(bf16[4096,768]{1,0:T(8,128)(2,1)} %get-tuple-element.40, bf16[4096,576]{1,0:T(8,128)(2,1)} %get-tuple-element.35), kind=kOutput, calls=%fused_computation.58 | convolution fusion | flops 3623878656 | bytes 12779520 | tf_op jit(solution)/shard_map/td,tc->dc/dot_general | solution.py:830
  632.3 14.2 %reduce-scatter.37.cloned.1.call-done = f32[96,9]{1,0:T(8,128)} async-done(((f32[768,9]{1,0:T(8,128)}), f32[96,9]{1,0:T(8,128)}) %reduce-scatter.37.cloned.1.call-update) | async-done | bytes 3472
  648.0 20.3 %reduce-scatter.23.cloned.1.call-done = bf16[1,96,192]{2,1,0:T(8,128)(2,1)} async-done(((bf16[4,96,192]{2,1,0:T(8,128)(2,1)}), bf16[1,96,192]{2,1,0:T(8,128)(2,1)}) %reduce-scatter.23.cloned.1.call-update) | async-done | bytes 36880 | tf_op jit(solution)/shard_map/reduce_scatter | solution.py:841
  669.8 23.5 %all-reduce.4 = f32[9,576]{1,0:T(8,128)S(1)} all-reduce(f32[9,576]{1,0:T(8,128)S(1)} %copy-done.5), channel_id=11, replica_groups=mesh['dp'=8,'tp'=4] {'dp'}, use_global_device_ids=true, to_apply=%region_5.7.clone | all-reduce | flops 5184 | bytes 41472
  695.6 18.0 %reduce-scatter.33.cloned.1.call-done = bf16[1,96,768]{2,1,0:T(8,128)(2,1)} async-done(((bf16[4,96,768]{2,1,0:T(8,128)(2,1)}), bf16[1,96,768]{2,1,0:T(8,128)(2,1)}) %reduce-scatter.33.cloned.1.call-update) | async-done | bytes 147472 | tf_op jit(solution)/shard_map/reduce_scatter | solution.py:841
  715.2 113.6 %all-gather.13.cloned.1.call-done = bf16[4096,768]{1,0:T(8,128)(2,1)} async-done(((bf16[1024,768]{1,0:T(8,128)(2,1)}), bf16[4096,768]{1,0:T(8,128)(2,1)}) %all-gather.13.cloned.1.call-update) | async-done | bytes 6291472 | tf_op jit(solution)/shard_map/all_gather | solution.py:824
  828.8 48.1 %reduce-scatter.35.cloned.1.call-done = f32[1152,4]{1,0:T(8,128)} async-done(((f32[4608,4]{1,0:T(8,128)}), f32[1152,4]{1,0:T(8,128)}) %reduce-scatter.35.cloned.1.call-update) | async-done | bytes 18448
  878.2 9.2 all-gather.7
  888.8 17.1 %psum.7 = f32[32,96]{1,0:T(8,128)S(1)} all-reduce(f32[32,96]{1,0:T(8,128)S(1)} %fusion.2), channel_id=1, replica_groups=mesh['dp'=8,'tp'=4] {'tp'}, use_global_device_ids=true, to_apply=%region_3.5 | all-reduce | flops 3072 | bytes 24576 | tf_op jit(solution)/shard_map/psum | solution.py:866
  911.0 9.3 %reduce-scatter.19.cloned.1.call-done = f32[96,576]{1,0:T(8,128)} async-done(((f32[768,576]{1,0:T(8,128)}), f32[96,576]{1,0:T(8,128)}) %reduce-scatter.19.cloned.1.call-update) | async-done | bytes 221200 | tf_op jit(solution)/shard_map/reduce_scatter | solution.py:831
  920.3 5.9 copy.49
  (115 shorter events, 42.5 us)
Async XLA Ops:
  7.2 49.6 %copy-start.10 = (s32[32]{0:T(128)S(1)}, s32[32]{0:T(128)}, u32[]{:S(2)}) copy-start(s32[32]{0:T(128)} %param.20) | copy-start | bytes 388
  7.2 49.6 %copy-start.9 = (s32[32]{0:T(128)S(1)}, s32[32]{0:T(128)}, u32[]{:S(2)}) copy-start(s32[32]{0:T(128)} %param.21) | copy-start | bytes 388
  7.2 196.9 %all-gather.15.cloned.1.call-start = ((), (), s32[]{:S(2)}) async-start(), calls=%async_computation.23 | async-start | bytes 1474560 | tf_op jit(solution)/shard_map/all_gather | solution.py:789
  7.9 196.2 %all-gather.17.cloned.1.call-start = ((), (), s32[]{:S(2)}) async-start(), calls=%async_computation.24 | async-start | bytes 5308416 | tf_op jit(solution)/shard_map/all_gather | solution.py:781
  8.9 53.2 %copy-start.2 = (bf16[768,1152]{1,0:T(8,128)(2,1)S(1)}, bf16[768,1152]{1,0:T(8,128)(2,1)}, u32[]{:S(2)}) copy-start(bf16[768,1152]{1,0:T(8,128)(2,1)} %param.24) | copy-start | bytes 5308420
  31.7 172.4 %all-gather.19.cloned.1.call-start = ((), (), s32[]{:S(2)}) async-start(), calls=%async_computation.25 | async-start | bytes 5308416 | tf_op jit(solution)/shard_map/all_gather | solution.py:781
  56.0 19.7 %copy-start.8 = (bf16[9,576]{1,0:T(8,128)(2,1)S(1)}, bf16[9,576]{1,0:T(8,128)(2,1)}, u32[]{:S(2)}) copy-start(bf16[9,576]{1,0:T(8,128)(2,1)} %param.26) | copy-start | bytes 31108
  56.0 20.4 %copy-start.3 = (bf16[768,576]{0,1:T(8,128)(2,1)S(1)}, bf16[768,576]{0,1:T(8,128)(2,1)}, u32[]{:S(2)}) copy-start(bf16[768,576]{0,1:T(8,128)(2,1)} %param.25) | copy-start | bytes 2654212
  138.6 4.0 copy-start
  142.8 1.4 copy-start.1
  145.9 3.8 copy-start.7
  145.9 55.8 %all-to-all-start = ((bf16[4,1280,192]{1,2,0:T(8,128)(2,1)}), bf16[4,1280,192]{1,2,0:T(8,128)(2,1)S(1)}, u32[]{:S(2)}, u32[]{:S(2)}) async-start(bf16[4,1280,192]{1,2,0:T(8,128)(2,1)} %pad_maximum_fusion), calls=%async_computation | async-start | bytes 3932160 | tf_op jit(solution)/shard_map/all_to_all | solution.py:814
  149.6 286.8 %reduce-scatter.29.cloned.1.call-start = ((), (), s32[]{:S(2)}) async-start(), calls=%async_computation.20 | async-start | bytes 245760 | tf_op jit(solution)/shard_map/reduce_scatter | solution.py:846
  312.6 125.6 %reduce-scatter.21.cloned.1.call-start = ((), (), s32[]{:S(2)}) async-start(), calls=%async_computation.16 | async-start | bytes 1769472 | tf_op jit(solution)/shard_map/reduce_scatter | solution.py:840
  313.2 125.6 %reduce-scatter.25.cloned.1.call-start = ((), (), s32[]{:S(2)}) async-start(), calls=%async_computation.18 | async-start | bytes 5308416 | tf_op jit(solution)/shard_map/reduce_scatter | solution.py:840
  313.8 181.6 %reduce-scatter.31.cloned.1.call-start = ((), (), s32[]{:S(2)}) async-start(), calls=%async_computation.21 | async-start | bytes 5308416 | tf_op jit(solution)/shard_map/reduce_scatter | solution.py:840
  314.5 293.9 %reduce-scatter.17.cloned.1.call-start = ((), (), s32[]{:S(2)}) async-start(), calls=%async_computation.14 | async-start | bytes 7864320 | tf_op jit(solution)/shard_map/reduce_scatter | solution.py:829
  400.0 26.5 %copy-start.4 = (bf16[768,576]{0,1:T(8,128)(2,1)S(1)}, bf16[768,576]{0,1:T(8,128)(2,1)}, u32[]{:S(2)}) copy-start(bf16[768,576]{0,1:T(8,128)(2,1)} %param.25) | copy-start | bytes 2654212
  436.3 210.2 %reduce-scatter.37.cloned.1.call-start = ((), (), s32[]{:S(2)}) async-start(), calls=%async_computation.27 | async-start | bytes 442368
  438.1 230.1 %reduce-scatter.23.cloned.1.call-start = ((), (), s32[]{:S(2)}) async-start(), calls=%async_computation.17 | async-start | bytes 245760 | tf_op jit(solution)/shard_map/reduce_scatter | solution.py:841
  438.7 255.3 %reduce-scatter.27.cloned.1.call-start = ((), (), s32[]{:S(2)}) async-start(), calls=%async_computation.19 | async-start | bytes 737280 | tf_op jit(solution)/shard_map/reduce_scatter | solution.py:841
  439.4 274.1 %reduce-scatter.33.cloned.1.call-start = ((), (), s32[]{:S(2)}) async-start(), calls=%async_computation.22 | async-start | bytes 737280 | tf_op jit(solution)/shard_map/reduce_scatter | solution.py:841
  495.3 333.5 %all-gather.13.cloned.1.call-start = ((), (), s32[]{:S(2)}) async-start(), calls=%async_computation.13 | async-start | bytes 7864320 | tf_op jit(solution)/shard_map/all_gather | solution.py:824
  496.1 380.8 %reduce-scatter.35.cloned.1.call-start = ((), (), s32[]{:S(2)}) async-start(), calls=%async_computation.26 | async-start | bytes 2949120
  608.4 9.3 copy-start.6
  620.3 300.0 %reduce-scatter.19.cloned.1.call-start = ((), (), s32[]{:S(2)}) async-start(), calls=%async_computation.15 | async-start | bytes 2211840 | tf_op jit(solution)/shard_map/reduce_scatter | solution.py:831
  630.4 0.7 copy-start.11
  630.4 39.4 %copy-start.5 = (f32[9,576]{1,0:T(8,128)S(1)}, f32[9,576]{1,0:T(8,128)}, u32[]{:S(2)}) copy-start(f32[9,576]{1,0:T(8,128)} %get-tuple-element.41) | copy-start | bytes 62212
Sparse Core Ops, SparseCore 0:
  9.6 45.2 all-gather.14
  56.7 38.2 all-gather.16
  96.9 38.8 all-gather.18
  312.7 28.2 reduce-scatter.28
  344.1 36.7 reduce-scatter.20
  384.2 53.7 reduce-scatter.24
  441.5 53.7 reduce-scatter.30
  497.6 110.7 reduce-scatter.16
  612.0 34.4 reduce-scatter.36
  648.6 19.5 reduce-scatter.22
  670.5 20.3 reduce-scatter.26
  693.1 20.4 reduce-scatter.32
  715.2 113.6 all-gather.12
  831.0 45.8 reduce-scatter.34
  880.7 39.5 reduce-scatter.18
